TPU v7x, 32 devices: a whole 2x2x4 slice. The times are simulated.
32 devices in a mesh: vol: 8 (over z, y), pix: 4 (over x, core).
Axes of the slice: x: 2, y: 2, z: 4, core: 2. Of those that a mesh axis runs over, the one named last changes fastest.
Arguments:
- kernel: bfloat16 [524288, 128], P(('vol', 'pix')), may hold values from 0 to 0.25
- pressure: bfloat16 [524288], P(('vol', 'pix')), may hold values from 0.049804688 to 2
- velocity: bfloat16 [524288], P(('vol', 'pix')), may hold values from -4 to 4
- entry_slot: int32 [32, 16384], P(('vol', 'pix')), may hold values from 0 to 1023, never falling along the last dimension, each value on 1 to 32 neighbouring positions
- slot_tile: int32 [32, 1024], P(('vol', 'pix')), may hold values from 0 to 8191, as said below
- tile_owner: int32 [8192], replicated, may hold values from 0 to 3, as said below
Outputs:
- owned_tiles: float32 [16384, 256], P(('vol', 'pix'))
- shell_map: float32 [8192, 256], P('vol')
Inputs may be any that keep to these rules, and one draw needn't show every extreme that they name: `entry_slot`: for each device the slot numbers never fall along its 16384 crossings; every slot has at least one crossing and at most 32. `tile_owner`: within every block of 1024 consecutive tiles each pix index owns 256 // 2 to 512 tiles, and one owner of each block owns exactly 512. `slot_tile`: the 1024 tiles of one device are distinct; at most 64 of them belong to any one owning device (vol index t // 1024, pix index tile_owner[t]), and one owning device gets exactly 64 from every device.
All inputs are finite; a program needn't handle non-finite values.
Results may differ from a plain program's by a relative error of at most 0.0003.
Values sent between devices are 32-bit elements; how exact they have to be, the bound alone decides.
No kernel may reach another device: no remote copies, remote signals or barrier semaphores. Data moves between devices by JAX's collectives and lax.ppermute only.
A program may use at most 64 MiB of HBM per device.

v0:
```python
import functools

import jax
import jax.numpy as jnp
from jax import lax
from jax.experimental import pallas as pl
from jax.experimental.pallas import tpu as pltpu
from jax.sharding import PartitionSpec as P


LANES = 128
HEAD = 8
ROOM = pltpu.CompilerParams(vmem_limit_bytes=16 << 20)
GROUP = 256
WINDOW = 40


SMEM = pl.BlockSpec(memory_space=pltpu.SMEM)
VMEM = pl.BlockSpec(memory_space=pltpu.VMEM)
ANY = pl.BlockSpec(memory_space=pl.ANY)
HBM = pl.BlockSpec(memory_space=pltpu.HBM)


def iota(shape, axis):
    return lax.broadcasted_iota(jnp.int32, shape, axis)


def nt_dot(a, b):
    return lax.dot_general(a, b, (((1,), (1,)), ((), ())), preferred_element_type=jnp.float32)


def dot(a, b):
    return jnp.dot(a, b, preferred_element_type=jnp.float32)


def ones_where(mask):
    return jnp.where(mask, 1.0, 0.0).astype(jnp.bfloat16)


def running_counts(marks, rows):
    total = marks.shape[0]
    upper = ones_where(iota((LANES, LANES), 0) <= iota((LANES, LANES), 1))
    row, column = iota((total, total), 0), iota((total, total), 1)
    earlier = ones_where((column < row) & (row // rows == column // rows))
    before = dot(earlier, marks).astype(jnp.bfloat16)
    return dot(marks, upper) + dot(before, jnp.ones((LANES, LANES), jnp.bfloat16))


def plan_kernel(vols, block, cap, me_ref, tile_ref, slot_ref, place_ref, ends_ref, head_ref):
    lane = iota((HEAD, LANES), 1)
    line = iota((HEAD, LANES), 0)
    slots = slot_ref[...]
    ends = ones_where(((line == 0) & (lane == 0)) | ((line == 1) & (lane == LANES - 1)))
    high = nt_dot(ends, (slots // 64).astype(jnp.float32).astype(jnp.bfloat16))
    low = nt_dot(ends, (slots % 64).astype(jnp.float32).astype(jnp.bfloat16))
    ends_ref[...] = (high * 64.0 + low).astype(jnp.int32)

    me = me_ref[0]
    tiles = tile_ref[...]
    rows = tiles.shape[0]
    vol = tiles // block
    local = tiles - vol * block + 1
    marks = jnp.concatenate([jnp.where(vol == i, 1.0, 0.0) for i in range(vols)], axis=0)
    counts = running_counts(marks.astype(jnp.bfloat16), rows) * marks
    place = jnp.zeros((rows, LANES), jnp.float32)
    for i in range(vols):
        place = place + counts[i * rows : (i + 1) * rows]
    place = place.astype(jnp.int32) - 1
    fits = place < cap
    bucket = vol ^ me
    place_ref[...] = jnp.where(fits, bucket * (cap + HEAD) + place, vols * (cap + HEAD))
    spilled = jnp.sum(jnp.where(fits, 0.0, 1.0), axis=(0, 1), keepdims=True)
    lists = -(-cap // LANES)
    width = lists * LANES
    high = (local // 64).astype(jnp.float32)
    low = (local % 64).astype(jnp.float32)
    ids = jnp.zeros((2 * vols, width), jnp.float32)
    which = iota((vols, LANES), 0)
    for r in range(rows):
        here = (bucket[r : r + 1] == which) & fits[r : r + 1]
        parts = jnp.concatenate(
            [jnp.where(here, high[r : r + 1], 0.0), jnp.where(here, low[r : r + 1], 0.0)], axis=0
        )
        spots = ones_where(iota((width, LANES), 0) == place[r : r + 1])
        ids = ids + nt_dot(parts.astype(jnp.bfloat16), spots)
    ids = ids[:vols] * 64.0 + ids[vols:] - 1.0
    for k in range(vols):
        head = jnp.where(line == lists, jnp.broadcast_to(spilled, (HEAD, LANES)), 0.0)
        for i in range(lists):
            head = jnp.where(line == i, ids[k : k + 1, i * LANES : (i + 1) * LANES], head)
        head_ref[k * HEAD : (k + 1) * HEAD, :] = head


def plan(me, tiles, slot, vols, block, cap):
    rows = tiles.shape[0]
    return pl.pallas_call(
        functools.partial(plan_kernel, vols, block, cap),
        in_specs=[SMEM, VMEM, VMEM],
        out_specs=[VMEM, VMEM, VMEM],
        out_shape=[
            jax.ShapeDtypeStruct((rows, LANES), jnp.int32),
            jax.ShapeDtypeStruct((HEAD, slot.shape[0]), jnp.int32),
            jax.ShapeDtypeStruct((vols * HEAD, LANES), jnp.float32),
        ],
        compiler_params=ROOM,
        name="plan",
    )(me, tiles, slot)


def project_kernel(steps, vols, cap, ends_ref, place_ref, kernel_hbm, factor_ref, slot_ref, head_ref, *rest):
    outs, (kernel_ref, partial_ref, stage_ref, factor_s, in_sem) = rest[:vols], rest[vols:]
    entries, _ = kernel_ref.shape
    part = entries // steps
    groups = part // GROUP
    lines = GROUP // LANES
    slots = place_ref.shape[0]
    total = entries // LANES
    size = cap + HEAD

    def load(step):
        piece = pl.ds(pl.multiple_of(step * part, part), part)
        return pltpu.make_async_copy(kernel_hbm.at[piece], kernel_ref.at[piece], in_sem.at[step])

    for step in range(steps):
        load(step).start()
    partial_ref[...] = jnp.zeros_like(partial_ref)
    stage_ref[...] = jnp.zeros_like(stage_ref)
    factor_s[...] = factor_ref[...].astype(jnp.float32)
    line = iota((WINDOW, LANES), 0)

    def first(group):
        return ends_ref[group * lines] & -8

    def reach(group):
        return ends_ref[total + group * lines + lines - 1] - first(group)

    def add(group, base):
        row = []
        for r in range(lines):
            at = pl.ds(group * lines + r, 1)
            row.append(jnp.where(line == slot_ref[at, :] - base, factor_s[at, :], 0.0))
        weights = jnp.concatenate(row, axis=1).astype(jnp.bfloat16)
        sums = dot(weights, kernel_ref[pl.ds(pl.multiple_of(group * GROUP, GROUP), GROUP), :])
        partial_ref[pl.ds(pl.multiple_of(base, 8), WINDOW), :] += sums

    def turn(step, most):
        load(step).wait()
        for g in range(groups):
            group = step * groups + g
            add(group, first(group))
            most = jnp.maximum(most, reach(group))
        return most

    most = lax.fori_loop(0, steps, turn, 0)

    @pl.when(most >= WINDOW)
    def _():
        def more(group, carry):
            def again(w, inner):
                add(group, first(group) + w * WINDOW)
                return inner

            return lax.fori_loop(1, reach(group) // WINDOW + 1, again, carry)

        lax.fori_loop(0, steps * groups, more, 0)

    unroll = 16

    def move(i, carry):
        for u in range(unroll):
            s = i * unroll + u
            stage_ref[pl.ds(place_ref[s], 1), :] = partial_ref[pl.ds(s, 1), :]
        return carry

    lax.fori_loop(0, slots // unroll, move, 0)
    for k in range(vols):
        outs[k][:cap, :] = stage_ref[k * size : k * size + cap, :]
        outs[k][cap:, :] = head_ref[k * HEAD : (k + 1) * HEAD, :]


def project(kernel, factor, slot, ends, place, head, vols, cap):
    entries, pixels = kernel.shape
    slots = place.shape[0]
    steps = 4
    size = cap + HEAD
    return pl.pallas_call(
        functools.partial(project_kernel, steps, vols, cap),
        in_specs=[SMEM, SMEM, HBM, VMEM, VMEM, VMEM],
        out_specs=[VMEM] * vols,
        out_shape=[jax.ShapeDtypeStruct((size, pixels), jnp.float32)] * vols,
        scratch_shapes=[
            pltpu.VMEM((entries, pixels), kernel.dtype),
            pltpu.VMEM((slots + WINDOW, pixels), jnp.float32),
            pltpu.VMEM((vols * size + HEAD, pixels), jnp.float32),
            pltpu.VMEM(factor.shape, jnp.float32),
            pltpu.SemaphoreType.DMA((steps,)),
        ],
        compiler_params=ROOM,
        name="project",
    )(ends, place, kernel, factor, slot, head)


def split(x):
    high = x.astype(jnp.bfloat16)
    return high, (x - high.astype(jnp.float32)).astype(jnp.bfloat16)


def collect_kernel(count, cap, first, last, block, *refs):
    core_ref, refs = (refs[0], refs[1:]) if last else (None, refs)
    buckets, refs = refs[:count], refs[count:]
    held_ref, refs = (None, refs) if first else (refs[0], refs[1:])
    pixels = buckets[0].shape[1]
    lists = -(-cap // LANES)
    outs, rows_s = refs[:-1], refs[-1]
    flag = jnp.zeros((HEAD, pixels), jnp.float32)
    ids = []
    for b, bucket in enumerate(buckets):
        rows_s[b] = jnp.concatenate(split(bucket[:cap, :]), axis=1)
        head = bucket[cap:, :]
        flag = flag + head[lists : lists + 1]
        names = [head[i : i + 1] for i in range(lists)]
        ids.append(jnp.concatenate(names, axis=1)[:, :cap].astype(jnp.int32))
    if held_ref is not None:
        flag = flag + held_ref[block:, :]

    def total(t, rows):
        sums = jnp.zeros((rows, 2 * pixels), jnp.float32)
        for b in range(count):
            sums = sums + dot(ones_where(iota((rows, cap), 0) + t == ids[b]), rows_s[b])
        sums = sums[:, :pixels] + sums[:, pixels:]
        return sums if held_ref is None else sums + held_ref[t : t + rows, :]

    chunk = 256
    if not last:
        for t in range(0, block, chunk):
            outs[0][t : t + chunk, :] = total(t, chunk)
        outs[0][block:, :] = flag
        return
    keep_ref, send_ref = outs
    lower = core_ref[0] == 0
    half = block // 2
    for t in range(0, half, chunk):
        one, two = total(t, chunk), total(t + half, chunk)
        keep_ref[t : t + chunk, :] = jnp.where(lower, one, two)
        send_ref[t : t + chunk, :] = jnp.where(lower, two, one)
    keep_ref[half:, :] = flag
    send_ref[half:, :] = flag


def collect(buckets, held, core, cap, block):
    pixels = buckets[0].shape[1]
    last = core is not None
    args = ([core] if last else []) + list(buckets) + ([] if held is None else [held])
    rows = block // 2 + HEAD if last else block + HEAD
    out = jax.ShapeDtypeStruct((rows, pixels), jnp.float32)
    return pl.pallas_call(
        functools.partial(collect_kernel, len(buckets), cap, held is None, last, block),
        in_specs=([SMEM] if last else []) + [VMEM] * (len(args) - last),
        out_specs=[VMEM] * 2 if last else VMEM,
        out_shape=[out] * 2 if last else out,
        scratch_shapes=[pltpu.VMEM((len(buckets), cap, 2 * pixels), jnp.bfloat16)],
        compiler_params=ROOM,
        name="collect_last" if last else "collect",
    )(*args)


def owner_kernel(most, pix_ref, owner_ref, row_ref):
    owners = owner_ref[...]
    rows = owners.shape[0]
    mine = owners == pix_ref[0]
    marks = jnp.where(mine, 1.0, 0.0)
    rank = running_counts(marks.astype(jnp.bfloat16), rows).astype(jnp.int32) - 1
    index = iota((rows, LANES), 0) * LANES + iota((rows, LANES), 1) + 1
    found = jnp.zeros((HEAD, most), jnp.float32)
    part = iota((HEAD, LANES), 0)
    for r in range(rows):
        here = mine[r : r + 1]
        high = jnp.where(here, (index[r : r + 1] // 64).astype(jnp.float32), 0.0)
        low = jnp.where(here, (index[r : r + 1] % 64).astype(jnp.float32), 0.0)
        parts = jnp.where(part == 0, high, jnp.where(part == 1, low, 0.0))
        spots = ones_where(iota((most, LANES), 0) == rank[r : r + 1])
        found = found + nt_dot(parts.astype(jnp.bfloat16), spots)
    tile = (found[0:1] * 64.0 + found[1:2]).astype(jnp.int32) - 1
    tile = jnp.where(tile < 0, rows * LANES, tile)
    row_ref[...] = jnp.broadcast_to(tile, (HEAD, most))


def owned_rows(pix, owners, most):
    return pl.pallas_call(
        functools.partial(owner_kernel, most),
        in_specs=[SMEM, VMEM],
        out_specs=VMEM,
        out_shape=jax.ShapeDtypeStruct((HEAD, most), jnp.int32),
        compiler_params=ROOM,
        name="owned_rows",
    )(pix, owners)


def finish_kernel(channel, core_ref, row_ref, mine_ref, other_ref, *rest):
    owned_ref, map_ref, full_ref, own_ref = rest[-4:]
    half, pixels = mine_ref.shape[0] - HEAD, mine_ref.shape[1]
    columns = slice(channel * pixels, (channel + 1) * pixels)
    core = core_ref[0]
    for at, part in ((core, mine_ref), (1 - core, other_ref)):
        at = pl.ds(pl.multiple_of(at * half, half), half)
        value = part[:half, :]
        full_ref[at, :] = value
        map_ref[at, columns] = value
    full_ref[2 * half :, :] = jnp.zeros((HEAD, pixels), jnp.float32)
    unroll = 16

    def move(i, carry):
        for u in range(unroll):
            r = i * unroll + u
            own_ref[pl.ds(r, 1), :] = full_ref[pl.ds(row_ref[r], 1), :]
        return carry

    lax.fori_loop(0, own_ref.shape[0] // unroll, move, 0)
    owned_ref[:, columns] = own_ref[...]


def finish(channel, core, rows, mine, other, before):
    block, pixels = 2 * (mine.shape[0] - HEAD), mine.shape[1]
    return pl.pallas_call(
        functools.partial(finish_kernel, channel),
        in_specs=[SMEM, SMEM, VMEM, VMEM] + [VMEM] * len(before),
        out_specs=[VMEM, VMEM],
        out_shape=[
            jax.ShapeDtypeStruct((rows.shape[0], 2 * pixels), jnp.float32),
            jax.ShapeDtypeStruct((block, 2 * pixels), jnp.float32),
        ],
        input_output_aliases={4: 0, 5: 1} if before else {},
        scratch_shapes=[
            pltpu.VMEM((block + HEAD, pixels), jnp.float32),
            pltpu.VMEM((rows.shape[0], pixels), jnp.float32),
        ],
        compiler_params=ROOM,
        name="finish",
    )(core, rows, mine, other, *before)


def shards(kernel, pressure, velocity, entry_slot, slot_tile, tile_owner):
    vols = lax.axis_size("vol")
    pixs = lax.axis_size("pix")
    vol = lax.axis_index("vol")
    pix = lax.axis_index("pix")
    entries, _ = kernel.shape
    slots = slot_tile.shape[1]
    block = tile_owner.shape[0] // vols
    most_owned = 2 * block // pixs
    most_rows = 2 * slots // vols
    scalar = lambda x: jnp.asarray(x, jnp.int32).reshape(1)
    tiles = slot_tile.reshape(slots // LANES, LANES)
    slot = entry_slot.reshape(entries // LANES, LANES)
    factors = [x.reshape(entries // LANES, LANES) for x in (pressure, velocity)]
    core = scalar(pix & 1)
    owners = lax.dynamic_slice_in_dim(
        tile_owner.reshape(vols, block // LANES, LANES), vol, 1
    )[0]
    rows = owned_rows(scalar(pix), owners, most_owned)[0]
    pairs = [(p, p ^ 1) for p in range(pixs)]

    def exchange(cap):
        place, ends, head = plan(scalar(vol), tiles, slot, vols, block, cap)
        place, ends = place.reshape(-1), ends.reshape(-1)
        arrived = []
        names = rows
        for channel, factor in enumerate(factors):
            if channel:
                factor, names = lax.optimization_barrier((factor, names))
            buckets = project(kernel, factor, slot, ends, place, head, vols, cap)
            if channel:
                arrived[0][0], *buckets = lax.optimization_barrier((arrived[0][0], *buckets))
            moved = {0: buckets[0]}
            for k in reversed(range(1, vols)):
                moved[k] = lax.ppermute(buckets[k], "vol", [(d, d ^ k) for d in range(vols)])
            arrived.append([moved[k] for k in range(vols)])
        half = vols // 2
        (near0, far0), (near1, far1) = [(a[:half], a[half:]) for a in arrived]

        def core_sum(near, far, held):
            if held is None:
                held = collect(near, None, None, cap, block)
            keep, send = collect(far, held, core, cap, block)
            return keep + lax.ppermute(send, "pix", pairs)

        def pix_sum(mine):
            step = 2
            while step < pixs:
                mine = mine + lax.ppermute(mine, "pix", [(p, p ^ step) for p in range(pixs)])
                step *= 2
            return mine

        mine0 = core_sum(near0, far0, None)
        mine0, near1[0] = lax.optimization_barrier((mine0, near1[0]))
        held1 = collect(near1, None, None, cap, block)
        mine0 = pix_sum(mine0)
        result = finish(0, core, names, mine0, lax.ppermute(mine0, "pix", pairs), ())
        far1[0], *result = lax.optimization_barrier((far1[0], *result))
        mine1 = pix_sum(core_sum(near1, far1, held1))
        result = finish(1, core, names, mine1, lax.ppermute(mine1, "pix", pairs), result)
        return mine0[block // 2, 0] > 0, *result

    result = exchange(most_rows * 23 // 32 // 8 * 8)

    def redo(state):
        unused, *full = exchange(most_rows)
        return jnp.zeros((), bool), *full

    _, owned, shell = lax.while_loop(lambda state: state[0], redo, result)
    return owned, shell


def solution(mesh):
    in_specs = (
        P(("vol", "pix"), None),
        P(("vol", "pix")),
        P(("vol", "pix")),
        P(("vol", "pix"), None),
        P(("vol", "pix"), None),
        P(),
    )
    out_specs = (P(("vol", "pix"), None), P("vol", None))
    return jax.shard_map(shards, mesh=mesh, in_specs=in_specs, out_specs=out_specs, check_vma=False)
```

profile of v0, /device:TPU:0, one launch (start us, length us, event | category | flops | bytes accessed | tf_op | source)
XLA Modules:
  0.0 77.1 jit_solution(8335393758139176222)
XLA Ops:
  0.7 1.6 %plan.3 = (s32[8,128]{1,0:T(8,128)S(1)}, s32[8,128]{1,0:T(8,128)S(1)}, f32[64,128]{1,0:T(8,128)S(1)}) custom-call(s32[1]{0:T(128)} %bitcast.4.me_ref, s32[8,128]{1,0:T(8,128)} %bitcast.37, s32[128,128]{1,0:T(8,128)} %bitcast.26), custom_call_target="tpu_custom_call" | custom-call | tf_op jit(solution)/shard_map/plan/pallas_call | solution.py:96
  2.3 4.6 %project.6 = (f32[192,128]{1,0:T(8,128)S(1)}, f32[192,128]{1,0:T(8,128)S(1)}, f32[192,128]{1,0:T(8,128)S(1)}, f32[192,128]{1,0:T(8,128)S(1)}, f32[192,128]{1,0:T...) custom-call(s32[1024]{0:T(1024)S(1)} %bitcast.24, s32[1024]{0:T(1024)S(1)} %bitcast.22, ...), custom_call_target="tpu_custom_call" | custom-call | tf_op jit(solution)/shard_map/project/pallas_call | solution.py:186
  6.9 3.1 %collective-permute-start.24 = (f32[192,128]{1,0:T(8,128)S(1)}, f32[192,128]{1,0:T(8,128)S(1)}, u32[]{:S(2)}, u32[]{:S(2)}) collective-permute-start(f32[192,128]{1,0:T(8,128)S(1)} %get-tuple-element.161), channel_id=1, source_target_pairs={{0,4},{4,0},{8,12},{12,8},{16,20},{20,16},{24,28},{28,24},{1,5},{5... | collective-permute-start | bytes 294920 | tf_op jit(solution)/shard_map/ppermute | solution.py:376
  9.9 1.6 %collective-permute-start.25 = (f32[192,128]{1,0:T(8,128)S(1)}, f32[192,128]{1,0:T(8,128)S(1)}, u32[]{:S(2)}, u32[]{:S(2)}) collective-permute-start(f32[192,128]{1,0:T(8,128)S(1)} %get-tuple-element.162), channel_id=1, source_target_pairs={{0,8},{4,12},{8,0},{12,4},{16,24},{20,28},{24,16},{28,20},{1,9},{5... | collective-permute-start | bytes 294920 | tf_op jit(solution)/shard_map/ppermute | solution.py:376
  11.5 2.6 %collective-permute-start.20 = (f32[192,128]{1,0:T(8,128)S(1)}, f32[192,128]{1,0:T(8,128)S(1)}, u32[]{:S(2)}, u32[]{:S(2)}) collective-permute-start(f32[192,128]{1,0:T(8,128)S(1)} %get-tuple-element.146), channel_id=1, source_target_pairs={{0,16},{4,20},{8,24},{12,28},{16,0},{20,4},{24,8},{28,12},{1,17},{... | collective-permute-start | bytes 294920 | tf_op jit(solution)/shard_map/ppermute | solution.py:376
  14.4 2.5 %collective-permute-start.22 = (f32[192,128]{1,0:T(8,128)S(1)}, f32[192,128]{1,0:T(8,128)S(1)}, u32[]{:S(2)}, u32[]{:S(2)}) collective-permute-start(f32[192,128]{1,0:T(8,128)S(1)} %get-tuple-element.148), channel_id=1, source_target_pairs={{0,24},{4,28},{8,16},{12,20},{16,8},{20,12},{24,0},{28,4},{1,25},{... | collective-permute-start | bytes 294920 | tf_op jit(solution)/shard_map/ppermute | solution.py:376
  16.8 2.3 %collective-permute-start.23 = (f32[192,128]{1,0:T(8,128)S(1)}, f32[192,128]{1,0:T(8,128)S(1)}, u32[]{:S(2)}, u32[]{:S(2)}) collective-permute-start(f32[192,128]{1,0:T(8,128)S(1)} %get-tuple-element.149), channel_id=1, source_target_pairs={{0,28},{4,24},{8,20},{12,16},{16,12},{20,8},{24,4},{28,0},{1,29},{... | collective-permute-start | bytes 294920 | tf_op jit(solution)/shard_map/ppermute | solution.py:376
  19.8 4.4 %project.7 = (f32[192,128]{1,0:T(8,128)S(1)}, f32[192,128]{1,0:T(8,128)S(1)}, f32[192,128]{1,0:T(8,128)S(1)}, f32[192,128]{1,0:T(8,128)S(1)}, f32[192,128]{1,0:T...) custom-call(s32[1024]{0:T(1024)S(1)} %bitcast.25, s32[1024]{0:T(1024)S(1)} %bitcast.23, ...), custom_call_target="tpu_custom_call" | custom-call | tf_op jit(solution)/shard_map/project/pallas_call | solution.py:186
  24.2 4.5 %collective-permute-done.26.refs_3_ = f32[192,128]{1,0:T(8,128)S(1)} collective-permute-done((f32[192,128]{1,0:T(8,128)S(1)}, f32[192,128]{1,0:T(8,128)S(1)}, u32[]{:S(2)}, u32[]{:S(2)}) %collective-permute-start.26) | collective-permute-done | bytes 98336 | tf_op jit(solution)/shard_map/ppermute | solution.py:376
  30.3 1.5 %collective-permute-done.27 = f32[520,128]{1,0:T(8,128)S(1)} collective-permute-done((f32[520,128]{1,0:T(8,128)S(1)}, f32[520,128]{1,0:T(8,128)S(1)}, u32[]{:S(2)}, u32[]{:S(2)}) %collective-permute-start.27) | collective-permute-done | bytes 266272 | tf_op jit(solution)/shard_map/ppermute | solution.py:385
  31.8 1.6 %collective-permute-start.28 = (f32[520,128]{1,0:T(8,128)S(1)}, f32[520,128]{1,0:T(8,128)S(1)}, u32[]{:S(2)}, u32[]{:S(2)}) collective-permute-start(f32[520,128]{1,0:T(8,128)S(1)} %add.28), channel_id=1, source_target_pairs={{0,2},{1,3},{2,0},{3,1},{4,6},{5,7},{6,4},{7,5},{8,10},{9,11},{10,... | collective-permute-start | bytes 798728 | tf_op jit(solution)/shard_map/ppermute | solution.py:390
  33.4 6.9 %collective-permute-done.28 = f32[520,128]{1,0:T(8,128)S(1)} collective-permute-done((f32[520,128]{1,0:T(8,128)S(1)}, f32[520,128]{1,0:T(8,128)S(1)}, u32[]{:S(2)}, u32[]{:S(2)}) %collective-permute-start.28) | collective-permute-done | bytes 266272 | tf_op jit(solution)/shard_map/ppermute | solution.py:390
  41.4 2.9 %collective-permute-start.35 = (f32[192,128]{1,0:T(8,128)S(1)}, f32[192,128]{1,0:T(8,128)S(1)}, u32[]{:S(2)}, u32[]{:S(2)}) collective-permute-start(f32[192,128]{1,0:T(8,128)S(1)} %get-tuple-element.178), channel_id=1, source_target_pairs={{0,8},{4,12},{8,0},{12,4},{16,24},{20,28},{24,16},{28,20},{1,9},{5... | collective-permute-start | bytes 294920 | tf_op jit(solution)/shard_map/ppermute | solution.py:376
  44.3 2.9 %collective-permute-start.29 = (f32[192,128]{1,0:T(8,128)S(1)}, f32[192,128]{1,0:T(8,128)S(1)}, u32[]{:S(2)}, u32[]{:S(2)}) collective-permute-start(f32[192,128]{1,0:T(8,128)S(1)} %get-tuple-element.169), channel_id=1, source_target_pairs={{0,16},{4,20},{8,24},{12,28},{16,0},{20,4},{24,8},{28,12},{1,17},{... | collective-permute-start | bytes 294920 | tf_op jit(solution)/shard_map/ppermute | solution.py:376
  47.2 2.6 %collective-permute-start.31 = (f32[192,128]{1,0:T(8,128)S(1)}, f32[192,128]{1,0:T(8,128)S(1)}, u32[]{:S(2)}, u32[]{:S(2)}) collective-permute-start(f32[192,128]{1,0:T(8,128)S(1)} %get-tuple-element.173), channel_id=1, source_target_pairs={{0,20},{4,16},{8,28},{12,24},{16,4},{20,0},{24,12},{28,8},{1,21},{... | collective-permute-start | bytes 294920 | tf_op jit(solution)/shard_map/ppermute | solution.py:376
  50.0 2.5 %collective-permute-start.32 = (f32[192,128]{1,0:T(8,128)S(1)}, f32[192,128]{1,0:T(8,128)S(1)}, u32[]{:S(2)}, u32[]{:S(2)}) collective-permute-start(f32[192,128]{1,0:T(8,128)S(1)} %get-tuple-element.174), channel_id=1, source_target_pairs={{0,24},{4,28},{8,16},{12,20},{16,8},{20,12},{24,0},{28,4},{1,25},{... | collective-permute-start | bytes 294920 | tf_op jit(solution)/shard_map/ppermute | solution.py:376
  52.7 3.1 %collective-permute-start.33 = (f32[192,128]{1,0:T(8,128)S(1)}, f32[192,128]{1,0:T(8,128)S(1)}, u32[]{:S(2)}, u32[]{:S(2)}) collective-permute-start(f32[192,128]{1,0:T(8,128)S(1)} %get-tuple-element.175), channel_id=1, source_target_pairs={{0,28},{4,24},{8,20},{12,16},{16,12},{20,8},{24,4},{28,0},{1,29},{... | collective-permute-start | bytes 294920 | tf_op jit(solution)/shard_map/ppermute | solution.py:376
  56.5 1.2 %finish.6 = (f32[512,256]{1,0:T(8,128)S(1)}, f32[1024,256]{1,0:T(8,128)S(1)}) custom-call(s32[1]{0:T(128)} %bitcast.3.refs_0_.core_ref, s32[512]{0:T(512)S(1)} %bitcast.34, f32[520,128]{1,0:T(8,128)S(1)} %add.29.mine_ref, f32[520,128]{1,0:T(8,128)S(1)} %collective-permute-done.30.other_ref), custom_call_target="tpu_custom_call" | custom-call | tf_op jit(solution)/shard_map/finish/pallas_call | solution.py:324
  57.7 4.5 %collective-permute-done.31.refs_2_ = f32[192,128]{1,0:T(8,128)S(1)} collective-permute-done((f32[192,128]{1,0:T(8,128)S(1)}, f32[192,128]{1,0:T(8,128)S(1)}, u32[]{:S(2)}, u32[]{:S(2)}) %collective-permute-start.31) | collective-permute-done | bytes 98336 | tf_op jit(solution)/shard_map/ppermute | solution.py:376
  63.0 1.5 %collective-permute-done.37 = f32[520,128]{1,0:T(8,128)S(1)} collective-permute-done((f32[520,128]{1,0:T(8,128)S(1)}, f32[520,128]{1,0:T(8,128)S(1)}, u32[]{:S(2)}, u32[]{:S(2)}) %collective-permute-start.37) | collective-permute-done | bytes 266272 | tf_op jit(solution)/shard_map/ppermute | solution.py:385
  64.6 1.5 %collective-permute-start.38 = (f32[520,128]{1,0:T(8,128)S(1)}, f32[520,128]{1,0:T(8,128)S(1)}, u32[]{:S(2)}, u32[]{:S(2)}) collective-permute-start(f32[520,128]{1,0:T(8,128)S(1)} %add.30), channel_id=1, source_target_pairs={{0,2},{1,3},{2,0},{3,1},{4,6},{5,7},{6,4},{7,5},{8,10},{9,11},{10,... | collective-permute-start | bytes 798728 | tf_op jit(solution)/shard_map/ppermute | solution.py:390
  66.1 7.0 %collective-permute-done.38 = f32[520,128]{1,0:T(8,128)S(1)} collective-permute-done((f32[520,128]{1,0:T(8,128)S(1)}, f32[520,128]{1,0:T(8,128)S(1)}, u32[]{:S(2)}, u32[]{:S(2)}) %collective-permute-start.38) | collective-permute-done | bytes 266272 | tf_op jit(solution)/shard_map/ppermute | solution.py:390
  74.7 1.2 %finish.7 = (f32[512,256]{1,0:T(8,128)S(1)}, f32[1024,256]{1,0:T(8,128)S(1)}) custom-call(s32[1]{0:T(128)} %bitcast.3.refs_0_.core_ref, s32[512]{0:T(512)S(1)} %bitcast.35, f32[520,128]{1,0:T(8,128)S(1)} %add.31.mine_ref, f32[520,128]{1,0:T(8,128)S(1)} %collective-permute-done.39.other_ref, ...), custom_call_target="tpu_custom_call", output_to_operand_aliasing={{0}: (4, {}), {1}: (5, {})} | custom-call | tf_op jit(solution)/shard_map/finish/pallas_call | solution.py:324
  76.0 0.9 %copy-done.1 = f32[1024,256]{1,0:T(8,128)} copy-done((f32[1024,256]{1,0:T(8,128)}, f32[1024,256]{1,0:T(8,128)S(1)}, u32[]{:S(2)}) %copy-start.1) | copy-done | bytes 1048600
  (48 shorter events, 6.6 us)
Async XLA Ops:
  0.6 19.2 %copy-start.3 = (s32[1,16384]{1,0:T(1,128)S(1)}, s32[1,16384]{1,0:T(1,128)}, u32[]{:S(2)}) copy-start(s32[1,16384]{1,0:T(1,128)} %param.11) | copy-start | bytes 196612
  0.7 19.2 %copy-start.7 = (bf16[16384]{0:T(1024)(128)(2,1)S(1)}, bf16[16384]{0:T(1024)(128)(2,1)}, u32[]{:S(2)}) copy-start(bf16[16384]{0:T(1024)(128)(2,1)} %param.10) | copy-start | bytes 98308
  6.9 10.0 %collective-permute-start.24 = (f32[192,128]{1,0:T(8,128)S(1)}, f32[192,128]{1,0:T(8,128)S(1)}, u32[]{:S(2)}, u32[]{:S(2)}) collective-permute-start(f32[192,128]{1,0:T(8,128)S(1)} %get-tuple-element.161), channel_id=1, source_target_pairs={{0,4},{4,0},{8,12},{12,8},{16,20},{20,16},{24,28},{28,24},{1,5},{5... | collective-permute-start | bytes 294920 | tf_op jit(solution)/shard_map/ppermute | solution.py:376
  9.9 9.2 %collective-permute-start.25 = (f32[192,128]{1,0:T(8,128)S(1)}, f32[192,128]{1,0:T(8,128)S(1)}, u32[]{:S(2)}, u32[]{:S(2)}) collective-permute-start(f32[192,128]{1,0:T(8,128)S(1)} %get-tuple-element.162), channel_id=1, source_target_pairs={{0,8},{4,12},{8,0},{12,4},{16,24},{20,28},{24,16},{28,20},{1,9},{5... | collective-permute-start | bytes 294920 | tf_op jit(solution)/shard_map/ppermute | solution.py:376
  11.5 17.9 %collective-permute-start.20 = (f32[192,128]{1,0:T(8,128)S(1)}, f32[192,128]{1,0:T(8,128)S(1)}, u32[]{:S(2)}, u32[]{:S(2)}) collective-permute-start(f32[192,128]{1,0:T(8,128)S(1)} %get-tuple-element.146), channel_id=1, source_target_pairs={{0,16},{4,20},{8,24},{12,28},{16,0},{20,4},{24,8},{28,12},{1,17},{... | collective-permute-start | bytes 294920 | tf_op jit(solution)/shard_map/ppermute | solution.py:376
  14.1 15.3 %collective-permute-start.21 = (f32[192,128]{1,0:T(8,128)S(1)}, f32[192,128]{1,0:T(8,128)S(1)}, u32[]{:S(2)}, u32[]{:S(2)}) collective-permute-start(f32[192,128]{1,0:T(8,128)S(1)} %get-tuple-element.147), channel_id=1, source_target_pairs={{0,20},{4,16},{8,28},{12,24},{16,4},{20,0},{24,12},{28,8},{1,21},{... | collective-permute-start | bytes 294920 | tf_op jit(solution)/shard_map/ppermute | solution.py:376
  14.4 15.1 %collective-permute-start.22 = (f32[192,128]{1,0:T(8,128)S(1)}, f32[192,128]{1,0:T(8,128)S(1)}, u32[]{:S(2)}, u32[]{:S(2)}) collective-permute-start(f32[192,128]{1,0:T(8,128)S(1)} %get-tuple-element.148), channel_id=1, source_target_pairs={{0,24},{4,28},{8,16},{12,20},{16,8},{20,12},{24,0},{28,4},{1,25},{... | collective-permute-start | bytes 294920 | tf_op jit(solution)/shard_map/ppermute | solution.py:376
  16.8 12.6 %collective-permute-start.23 = (f32[192,128]{1,0:T(8,128)S(1)}, f32[192,128]{1,0:T(8,128)S(1)}, u32[]{:S(2)}, u32[]{:S(2)}) collective-permute-start(f32[192,128]{1,0:T(8,128)S(1)} %get-tuple-element.149), channel_id=1, source_target_pairs={{0,28},{4,24},{8,20},{12,16},{16,12},{20,8},{24,4},{28,0},{1,29},{... | collective-permute-start | bytes 294920 | tf_op jit(solution)/shard_map/ppermute | solution.py:376
  19.1 9.5 %collective-permute-start.26 = (f32[192,128]{1,0:T(8,128)S(1)}, f32[192,128]{1,0:T(8,128)S(1)}, u32[]{:S(2)}, u32[]{:S(2)}) collective-permute-start(f32[192,128]{1,0:T(8,128)S(1)} %get-tuple-element.163), channel_id=1, source_target_pairs={{0,12},{4,8},{8,4},{12,0},{16,28},{20,24},{24,20},{28,16},{1,13},{... | collective-permute-start | bytes 294920 | tf_op jit(solution)/shard_map/ppermute | solution.py:376
  29.4 47.6 %copy-start.6 = (bf16[16384]{0:T(1024)(128)(2,1)S(1)}, bf16[16384]{0:T(1024)(128)(2,1)}, u32[]{:S(2)}) copy-start(bf16[16384]{0:T(1024)(128)(2,1)} %param.9) | copy-start | bytes 98308
  29.5 47.6 %copy-start.8 = (s32[1,1024]{1,0:T(1,128)S(1)}, s32[1,1024]{1,0:T(1,128)}, u32[]{:S(2)}) copy-start(s32[1,1024]{1,0:T(1,128)} %param.12) | copy-start | bytes 12292
  30.2 1.6 %collective-permute-start.27 = (f32[520,128]{1,0:T(8,128)S(1)}, f32[520,128]{1,0:T(8,128)S(1)}, u32[]{:S(2)}, u32[]{:S(2)}) collective-permute-start(f32[520,128]{1,0:T(8,128)S(1)} %get-tuple-element.165), channel_id=1, source_target_pairs={{0,1},{1,0},{2,3},{3,2},{4,5},{5,4},{6,7},{7,6},{8,9},{9,8},{10,11... | collective-permute-start | bytes 798728 | tf_op jit(solution)/shard_map/ppermute | solution.py:385
  31.8 8.5 %collective-permute-start.28 = (f32[520,128]{1,0:T(8,128)S(1)}, f32[520,128]{1,0:T(8,128)S(1)}, u32[]{:S(2)}, u32[]{:S(2)}) collective-permute-start(f32[520,128]{1,0:T(8,128)S(1)} %add.28), channel_id=1, source_target_pairs={{0,2},{1,3},{2,0},{3,1},{4,6},{5,7},{6,4},{7,5},{8,10},{9,11},{10,... | collective-permute-start | bytes 798728 | tf_op jit(solution)/shard_map/ppermute | solution.py:390
  40.4 16.1 %collective-permute-start.30 = (f32[520,128]{1,0:T(8,128)S(1)}, f32[520,128]{1,0:T(8,128)S(1)}, u32[]{:S(2)}, u32[]{:S(2)}) collective-permute-start(f32[520,128]{1,0:T(8,128)S(1)} %add.29.mine_ref), channel_id=1, source_target_pairs={{0,1},{1,0},{2,3},{3,2},{4,5},{5,4},{6,7},{7,6},{8,9},{9,8},{10,11... | collective-permute-start | bytes 798728 | tf_op jit(solution)/shard_map/ppermute | solution.py:398
  40.5 6.8 %collective-permute-start.34 = (f32[192,128]{1,0:T(8,128)S(1)}, f32[192,128]{1,0:T(8,128)S(1)}, u32[]{:S(2)}, u32[]{:S(2)}) collective-permute-start(f32[192,128]{1,0:T(8,128)S(1)} %get-tuple-element.177), channel_id=1, source_target_pairs={{0,4},{4,0},{8,12},{12,8},{16,20},{20,16},{24,28},{28,24},{1,5},{5... | collective-permute-start | bytes 294920 | tf_op jit(solution)/shard_map/ppermute | solution.py:376
  41.4 8.7 %collective-permute-start.35 = (f32[192,128]{1,0:T(8,128)S(1)}, f32[192,128]{1,0:T(8,128)S(1)}, u32[]{:S(2)}, u32[]{:S(2)}) collective-permute-start(f32[192,128]{1,0:T(8,128)S(1)} %get-tuple-element.178), channel_id=1, source_target_pairs={{0,8},{4,12},{8,0},{12,4},{16,24},{20,28},{24,16},{28,20},{1,9},{5... | collective-permute-start | bytes 294920 | tf_op jit(solution)/shard_map/ppermute | solution.py:376
  44.3 8.4 %collective-permute-start.36 = (f32[192,128]{1,0:T(8,128)S(1)}, f32[192,128]{1,0:T(8,128)S(1)}, u32[]{:S(2)}, u32[]{:S(2)}) collective-permute-start(f32[192,128]{1,0:T(8,128)S(1)} %get-tuple-element.179), channel_id=1, source_target_pairs={{0,12},{4,8},{8,4},{12,0},{16,28},{20,24},{24,20},{28,16},{1,13},{... | collective-permute-start | bytes 294920 | tf_op jit(solution)/shard_map/ppermute | solution.py:376
  44.3 13.4 %collective-permute-start.29 = (f32[192,128]{1,0:T(8,128)S(1)}, f32[192,128]{1,0:T(8,128)S(1)}, u32[]{:S(2)}, u32[]{:S(2)}) collective-permute-start(f32[192,128]{1,0:T(8,128)S(1)} %get-tuple-element.169), channel_id=1, source_target_pairs={{0,16},{4,20},{8,24},{12,28},{16,0},{20,4},{24,8},{28,12},{1,17},{... | collective-permute-start | bytes 294920 | tf_op jit(solution)/shard_map/ppermute | solution.py:376
  47.2 15.0 %collective-permute-start.31 = (f32[192,128]{1,0:T(8,128)S(1)}, f32[192,128]{1,0:T(8,128)S(1)}, u32[]{:S(2)}, u32[]{:S(2)}) collective-permute-start(f32[192,128]{1,0:T(8,128)S(1)} %get-tuple-element.173), channel_id=1, source_target_pairs={{0,20},{4,16},{8,28},{12,24},{16,4},{20,0},{24,12},{28,8},{1,21},{... | collective-permute-start | bytes 294920 | tf_op jit(solution)/shard_map/ppermute | solution.py:376
  50.0 12.2 %collective-permute-start.32 = (f32[192,128]{1,0:T(8,128)S(1)}, f32[192,128]{1,0:T(8,128)S(1)}, u32[]{:S(2)}, u32[]{:S(2)}) collective-permute-start(f32[192,128]{1,0:T(8,128)S(1)} %get-tuple-element.174), channel_id=1, source_target_pairs={{0,24},{4,28},{8,16},{12,20},{16,8},{20,12},{24,0},{28,4},{1,25},{... | collective-permute-start | bytes 294920 | tf_op jit(solution)/shard_map/ppermute | solution.py:376
  52.7 9.5 %collective-permute-start.33 = (f32[192,128]{1,0:T(8,128)S(1)}, f32[192,128]{1,0:T(8,128)S(1)}, u32[]{:S(2)}, u32[]{:S(2)}) collective-permute-start(f32[192,128]{1,0:T(8,128)S(1)} %get-tuple-element.175), channel_id=1, source_target_pairs={{0,28},{4,24},{8,20},{12,16},{16,12},{20,8},{24,4},{28,0},{1,29},{... | collective-permute-start | bytes 294920 | tf_op jit(solution)/shard_map/ppermute | solution.py:376
  63.0 1.6 %collective-permute-start.37 = (f32[520,128]{1,0:T(8,128)S(1)}, f32[520,128]{1,0:T(8,128)S(1)}, u32[]{:S(2)}, u32[]{:S(2)}) collective-permute-start(f32[520,128]{1,0:T(8,128)S(1)} %get-tuple-element.181), channel_id=1, source_target_pairs={{0,1},{1,0},{2,3},{3,2},{4,5},{5,4},{6,7},{7,6},{8,9},{9,8},{10,11... | collective-permute-start | bytes 798728 | tf_op jit(solution)/shard_map/ppermute | solution.py:385
  64.6 8.5 %collective-permute-start.38 = (f32[520,128]{1,0:T(8,128)S(1)}, f32[520,128]{1,0:T(8,128)S(1)}, u32[]{:S(2)}, u32[]{:S(2)}) collective-permute-start(f32[520,128]{1,0:T(8,128)S(1)} %add.30), channel_id=1, source_target_pairs={{0,2},{1,3},{2,0},{3,1},{4,6},{5,7},{6,4},{7,5},{8,10},{9,11},{10,... | collective-permute-start | bytes 798728 | tf_op jit(solution)/shard_map/ppermute | solution.py:390
  73.1 1.6 %collective-permute-start.39 = (f32[520,128]{1,0:T(8,128)S(1)}, f32[520,128]{1,0:T(8,128)S(1)}, u32[]{:S(2)}, u32[]{:S(2)}) collective-permute-start(f32[520,128]{1,0:T(8,128)S(1)} %add.31.mine_ref), channel_id=1, source_target_pairs={{0,1},{1,0},{2,3},{3,2},{4,5},{5,4},{6,7},{7,6},{8,9},{9,8},{10,11... | collective-permute-start | bytes 798728 | tf_op jit(solution)/shard_map/ppermute | solution.py:401
  (3 other events, 20.6 us)
where the time goes:
time: 78.5 us; the launch traced here: 77.1 us
  starting transfers between devices  30.6 us (39%)
  waiting for transfers between devices  26.7 us (34%)
  Pallas kernels  16.4 us (21%)
  local copies, waits for them, and re-layouts  1.68 us (2%)
  between operations  1.57 us (2%)
    ppermute x14, starting transfers between devices, exchange(): lax.ppermute(buckets[k], 'vol', [(d, d ^ k) for d in range(vols)])  27.2 us
    ppermute x2, waiting for transfers between devices, pix_sum(): lax.ppermute(mine, 'pix', [(p, p ^ step) for p in range(pixs)])  13.9 us
    ppermute x14, waiting for transfers between devices, exchange(): lax.ppermute(buckets[k], 'vol', [(d, d ^ k) for d in range(vols)])  9.4 us
    pallas_call x2, Pallas kernels, project(): pl.pallas_call(functools.partial(project_kernel, steps, vols, cap), in_sp...  8.93 us
    ppermute x2, starting transfers between devices, pix_sum(): lax.ppermute(mine, 'pix', [(p, p ^ step) for p in range(pixs)])  3.1 us
    ppermute x2, waiting for transfers between devices, core_sum(): return keep + lax.ppermute(send, 'pix', pairs)  3.06 us
    pallas_call x4, Pallas kernels, collect(): pl.pallas_call(functools.partial(collect_kernel, len(buckets), cap, held...  2.87 us
    pallas_call x2, Pallas kernels, finish(): pl.pallas_call(functools.partial(finish_kernel, channel), in_specs=[SMEM,...  2.38 us
  transfers between devices with their start and end apart: 20, of which 9 were waited for; matrix products, arithmetic and copies ran while one was open for 1% of the time, Pallas kernels for 10%

commit v1 on v0

--- a/solution.py
+++ b/solution.py
@@ -35,6 +35,10 @@
 
 def ones_where(mask):
     return jnp.where(mask, 1.0, 0.0).astype(jnp.bfloat16)
+
+
+def bytes_of(x):
+    return (x >> 8).astype(jnp.float32), (x & 255).astype(jnp.float32)
 
 
 def running_counts(marks, rows):
@@ -46,35 +50,56 @@
     return dot(marks, upper) + dot(before, jnp.ones((LANES, LANES), jnp.bfloat16))
 
 
-def plan_kernel(vols, block, cap, me_ref, tile_ref, slot_ref, place_ref, ends_ref, head_ref):
+class Room:
+    def __init__(self, vols, near, far, pool):
+        self.vols, self.near, self.far, self.pool = vols, near, far, pool
+        self.half = vols // 2
+        self.lists = -(-max(near, far, pool) // LANES)
+        self.sizes = [near] * self.half + [far] * self.half + ([pool] if pool else [])
+        self.starts = [sum(self.sizes[:k]) for k in range(len(self.sizes) + 1)]
+
+
+def plan_kernel(room, block, me_ref, tile_ref, slot_ref, place_ref, ends_ref, head_ref):
+    vols, half = room.vols, room.half
     lane = iota((HEAD, LANES), 1)
     line = iota((HEAD, LANES), 0)
     slots = slot_ref[...]
     ends = ones_where(((line == 0) & (lane == 0)) | ((line == 1) & (lane == LANES - 1)))
-    high = nt_dot(ends, (slots // 64).astype(jnp.float32).astype(jnp.bfloat16))
-    low = nt_dot(ends, (slots % 64).astype(jnp.float32).astype(jnp.bfloat16))
-    ends_ref[...] = (high * 64.0 + low).astype(jnp.int32)
+    high, low = bytes_of(slots)
+    ends_ref[...] = (
+        nt_dot(ends, high.astype(jnp.bfloat16)) * 256.0 + nt_dot(ends, low.astype(jnp.bfloat16))
+    ).astype(jnp.int32)
 
     me = me_ref[0]
     tiles = tile_ref[...]
     rows = tiles.shape[0]
     vol = tiles // block
-    local = tiles - vol * block + 1
     marks = jnp.concatenate([jnp.where(vol == i, 1.0, 0.0) for i in range(vols)], axis=0)
     counts = running_counts(marks.astype(jnp.bfloat16), rows) * marks
     place = jnp.zeros((rows, LANES), jnp.float32)
     for i in range(vols):
         place = place + counts[i * rows : (i + 1) * rows]
     place = place.astype(jnp.int32) - 1
-    fits = place < cap
     bucket = vol ^ me
-    place_ref[...] = jnp.where(fits, bucket * (cap + HEAD) + place, vols * (cap + HEAD))
-    spilled = jnp.sum(jnp.where(fits, 0.0, 1.0), axis=(0, 1), keepdims=True)
-    lists = -(-cap // LANES)
+    far = bucket >= half
+    fits = place < jnp.where(far, room.far, room.near)
+    start = jnp.where(far, half * room.near + (bucket - half) * room.far, bucket * room.near)
+    target = jnp.where(fits, start + place, room.starts[-1])
+    left = jnp.where(fits, 0.0, 1.0)
+    if room.pool:
+        extra = jnp.where(far, left, 0.0)
+        rank = running_counts(extra.astype(jnp.bfloat16), rows).astype(jnp.int32) - 1
+        pooled = (extra > 0) & (rank < room.pool)
+        target = jnp.where(pooled, room.starts[vols] + rank, target)
+        left = jnp.where(pooled, 0.0, left)
+    place_ref[...] = target
+    spilled = jnp.sum(left, axis=(0, 1), keepdims=True)
+    lists = room.lists
     width = lists * LANES
-    high = (local // 64).astype(jnp.float32)
-    low = (local % 64).astype(jnp.float32)
+    high, low = bytes_of(tiles - vol * block + 1)
+    pool_high, pool_low = bytes_of(tiles + 1)
     ids = jnp.zeros((2 * vols, width), jnp.float32)
+    pool_ids = jnp.zeros((HEAD, width), jnp.float32)
     which = iota((vols, LANES), 0)
     for r in range(rows):
         here = (bucket[r : r + 1] == which) & fits[r : r + 1]
@@ -83,39 +108,46 @@
         )
         spots = ones_where(iota((width, LANES), 0) == place[r : r + 1])
         ids = ids + nt_dot(parts.astype(jnp.bfloat16), spots)
-    ids = ids[:vols] * 64.0 + ids[vols:] - 1.0
-    for k in range(vols):
+        if room.pool:
+            parts = jnp.where(line == 0, pool_high[r : r + 1], jnp.where(line == 1, pool_low[r : r + 1], 0.0))
+            parts = jnp.where(pooled[r : r + 1], parts, 0.0)
+            spots = ones_where(iota((width, LANES), 0) == rank[r : r + 1])
+            pool_ids = pool_ids + nt_dot(parts.astype(jnp.bfloat16), spots)
+    ids = ids[:vols] * 256.0 + ids[vols:] - 1.0
+    pool_ids = pool_ids[0:1] * 256.0 + pool_ids[1:2] - 1.0
+    for k in range(len(room.sizes)):
+        names = ids[k : k + 1] if k < vols else pool_ids
         head = jnp.where(line == lists, jnp.broadcast_to(spilled, (HEAD, LANES)), 0.0)
         for i in range(lists):
-            head = jnp.where(line == i, ids[k : k + 1, i * LANES : (i + 1) * LANES], head)
+            head = jnp.where(line == i, names[:, i * LANES : (i + 1) * LANES], head)
         head_ref[k * HEAD : (k + 1) * HEAD, :] = head
 
 
-def plan(me, tiles, slot, vols, block, cap):
+def plan(me, tiles, slot, room, block):
     rows = tiles.shape[0]
     return pl.pallas_call(
-        functools.partial(plan_kernel, vols, block, cap),
+        functools.partial(plan_kernel, room, block),
         in_specs=[SMEM, VMEM, VMEM],
         out_specs=[VMEM, VMEM, VMEM],
         out_shape=[
             jax.ShapeDtypeStruct((rows, LANES), jnp.int32),
             jax.ShapeDtypeStruct((HEAD, slot.shape[0]), jnp.int32),
-            jax.ShapeDtypeStruct((vols * HEAD, LANES), jnp.float32),
+            jax.ShapeDtypeStruct((len(room.sizes) * HEAD, LANES), jnp.float32),
         ],
         compiler_params=ROOM,
         name="plan",
     )(me, tiles, slot)
 
 
-def project_kernel(steps, vols, cap, ends_ref, place_ref, kernel_hbm, factor_ref, slot_ref, head_ref, *rest):
-    outs, (kernel_ref, partial_ref, stage_ref, factor_s, in_sem) = rest[:vols], rest[vols:]
+def project_kernel(steps, room, named, ends_ref, place_ref, kernel_hbm, factor_ref, slot_ref, head_ref, *rest):
+    count = len(room.sizes)
+    outs, (kernel_ref, partial_ref, stage_ref, factor_s, in_sem) = rest[:count], rest[count:]
     entries, _ = kernel_ref.shape
     part = entries // steps
     groups = part // GROUP
     lines = GROUP // LANES
     slots = place_ref.shape[0]
     total = entries // LANES
-    size = cap + HEAD
 
     def load(step):
         piece = pl.ds(pl.multiple_of(step * part, part), part)
@@ -173,25 +205,26 @@
         return carry
 
     lax.fori_loop(0, slots // unroll, move, 0)
-    for k in range(vols):
-        outs[k][:cap, :] = stage_ref[k * size : k * size + cap, :]
-        outs[k][cap:, :] = head_ref[k * HEAD : (k + 1) * HEAD, :]
-
-
-def project(kernel, factor, slot, ends, place, head, vols, cap):
+    for k, size in enumerate(room.sizes):
+        outs[k][:size, :] = stage_ref[room.starts[k] : room.starts[k + 1], :]
+        if named:
+            outs[k][size:, :] = head_ref[k * HEAD : (k + 1) * HEAD, :]
+
+
+def project(kernel, factor, slot, ends, place, head, room, named):
     entries, pixels = kernel.shape
     slots = place.shape[0]
     steps = 4
-    size = cap + HEAD
+    sizes = [size + HEAD * named for size in room.sizes]
     return pl.pallas_call(
-        functools.partial(project_kernel, steps, vols, cap),
+        functools.partial(project_kernel, steps, room, named),
         in_specs=[SMEM, SMEM, HBM, VMEM, VMEM, VMEM],
-        out_specs=[VMEM] * vols,
-        out_shape=[jax.ShapeDtypeStruct((size, pixels), jnp.float32)] * vols,
+        out_specs=[VMEM] * len(sizes),
+        out_shape=[jax.ShapeDtypeStruct((size, pixels), jnp.float32) for size in sizes],
         scratch_shapes=[
             pltpu.VMEM((entries, pixels), kernel.dtype),
             pltpu.VMEM((slots + WINDOW, pixels), jnp.float32),
-            pltpu.VMEM((vols * size + HEAD, pixels), jnp.float32),
+            pltpu.VMEM((room.starts[-1] + HEAD, pixels), jnp.float32),
             pltpu.VMEM(factor.shape, jnp.float32),
             pltpu.SemaphoreType.DMA((steps,)),
         ],
@@ -205,28 +238,30 @@
     return high, (x - high.astype(jnp.float32)).astype(jnp.bfloat16)
 
 
-def collect_kernel(count, cap, first, last, block, *refs):
-    core_ref, refs = (refs[0], refs[1:]) if last else (None, refs)
-    buckets, refs = refs[:count], refs[count:]
+def collect_kernel(items, lists, first, last, block, arrays, scalars_ref, *refs):
+    inputs, refs = refs[:arrays], refs[arrays:]
     held_ref, refs = (None, refs) if first else (refs[0], refs[1:])
-    pixels = buckets[0].shape[1]
-    lists = -(-cap // LANES)
-    outs, rows_s = refs[:-1], refs[-1]
+    pixels = inputs[0].shape[1]
+    outs, rows_s = refs[: 1 + last], refs[1 + last :]
     flag = jnp.zeros((HEAD, pixels), jnp.float32)
     ids = []
-    for b, bucket in enumerate(buckets):
-        rows_s[b] = jnp.concatenate(split(bucket[:cap, :]), axis=1)
-        head = bucket[cap:, :]
-        flag = flag + head[lists : lists + 1]
-        names = [head[i : i + 1] for i in range(lists)]
-        ids.append(jnp.concatenate(names, axis=1)[:, :cap].astype(jnp.int32))
+    for value, step, head, size, index, pooled in items:
+        rows = inputs[value][index * step : index * step + size, :]
+        rows_s[len(ids)][...] = jnp.concatenate(split(rows), axis=1)
+        at = index * (size + HEAD) + size
+        heads = inputs[head][at : at + HEAD, :]
+        if not pooled:
+            flag = flag + heads[lists : lists + 1]
+        names = jnp.concatenate([heads[i : i + 1] for i in range(lists)], axis=1)[:, :size]
+        names = names.astype(jnp.int32)
+        ids.append(names - scalars_ref[0] * block if pooled else names)
     if held_ref is not None:
         flag = flag + held_ref[block:, :]
 
     def total(t, rows):
         sums = jnp.zeros((rows, 2 * pixels), jnp.float32)
-        for b in range(count):
-            sums = sums + dot(ones_where(iota((rows, cap), 0) + t == ids[b]), rows_s[b])
+        for names, values in zip(ids, rows_s):
+            sums = sums + dot(ones_where(iota((rows, names.shape[1]), 0) + t == names), values[...])
         sums = sums[:, :pixels] + sums[:, pixels:]
         return sums if held_ref is None else sums + held_ref[t : t + rows, :]
 
@@ -237,7 +272,7 @@
         outs[0][block:, :] = flag
         return
     keep_ref, send_ref = outs
-    lower = core_ref[0] == 0
+    lower = scalars_ref[1] == 0
     half = block // 2
     for t in range(0, half, chunk):
         one, two = total(t, chunk), total(t + half, chunk)
@@ -247,18 +282,27 @@
     send_ref[half:, :] = flag
 
 
-def collect(buckets, held, core, cap, block):
-    pixels = buckets[0].shape[1]
-    last = core is not None
-    args = ([core] if last else []) + list(buckets) + ([] if held is None else [held])
+def collect(parts, held, last, scalars, lists, block):
+    inputs, items = [], []
+    for values, head, size, count, pooled in parts:
+        places = []
+        for array in (values, head):
+            known = [i for i, other in enumerate(inputs) if other is array]
+            places.append(known[0] if known else len(inputs))
+            if not known:
+                inputs.append(array)
+        step = values.shape[0] // count
+        items += [(places[0], step, places[1], size, i, pooled) for i in range(count)]
+    pixels = inputs[0].shape[1]
+    args = [scalars, *inputs] + ([] if held is None else [held])
     rows = block // 2 + HEAD if last else block + HEAD
     out = jax.ShapeDtypeStruct((rows, pixels), jnp.float32)
     return pl.pallas_call(
-        functools.partial(collect_kernel, len(buckets), cap, held is None, last, block),
-        in_specs=([SMEM] if last else []) + [VMEM] * (len(args) - last),
+        functools.partial(collect_kernel, tuple(items), lists, held is None, last, block, len(inputs)),
+        in_specs=[SMEM] + [VMEM] * (len(args) - 1),
         out_specs=[VMEM] * 2 if last else VMEM,
         out_shape=[out] * 2 if last else out,
-        scratch_shapes=[pltpu.VMEM((len(buckets), cap, 2 * pixels), jnp.bfloat16)],
+        scratch_shapes=[pltpu.VMEM((item[3], 2 * pixels), jnp.bfloat16) for item in items],
         compiler_params=ROOM,
         name="collect_last" if last else "collect",
     )(*args)
@@ -360,29 +404,55 @@
     rows = owned_rows(scalar(pix), owners, most_owned)[0]
     pairs = [(p, p ^ 1) for p in range(pixs)]
 
-    def exchange(cap):
-        place, ends, head = plan(scalar(vol), tiles, slot, vols, block, cap)
+    scalars = jnp.stack([vol, pix & 1]).astype(jnp.int32)
+    hops = [1 << i for i in reversed(range((vols // 2).bit_length() - 1))]
+
+    def send(x, k):
+        return lax.ppermute(x, "vol", [(d, d ^ k) for d in range(vols)])
+
+    def exchange(room):
+        place, ends, head = plan(scalar(vol), tiles, slot, room, block)
         place, ends = place.reshape(-1), ends.reshape(-1)
-        arrived = []
+        half = vols // 2
+        arrived, pools = [], []
         names = rows
         for channel, factor in enumerate(factors):
             if channel:
                 factor, names = lax.optimization_barrier((factor, names))
-            buckets = project(kernel, factor, slot, ends, place, head, vols, cap)
+            parts = project(kernel, factor, slot, ends, place, head, room, channel == 0)
             if channel:
-                arrived[0][0], *buckets = lax.optimization_barrier((arrived[0][0], *buckets))
-            moved = {0: buckets[0]}
+                arrived[0][0], *parts = lax.optimization_barrier((arrived[0][0], *parts))
+            if room.pool:
+                pool = send(parts[vols], half)
+                if channel:
+                    parts[0], pools[0] = lax.optimization_barrier((parts[0], pools[0]))
+                pools.append(pool)
+            moved = {0: parts[0]}
             for k in reversed(range(1, vols)):
-                moved[k] = lax.ppermute(buckets[k], "vol", [(d, d ^ k) for d in range(vols)])
+                moved[k] = send(parts[k], k)
             arrived.append([moved[k] for k in range(vols)])
-        half = vols // 2
-        (near0, far0), (near1, far1) = [(a[:half], a[half:]) for a in arrived]
-
-        def core_sum(near, far, held):
-            if held is None:
-                held = collect(near, None, None, cap, block)
-            keep, send = collect(far, held, core, cap, block)
-            return keep + lax.ppermute(send, "pix", pairs)
+
+        def spread(channel):
+            pool = pools[channel]
+            for k in hops:
+                pool = jnp.concatenate([pool, send(pool, k)], axis=0)
+            return pool
+
+        heads = arrived[0]
+        if room.pool:
+            pools[0] = spread(0)
+            pools[1] = spread(1)
+
+        def near(channel):
+            parts = [(arrived[channel][k], heads[k], room.near, 1, False) for k in range(half)]
+            return collect(parts, None, False, scalars, room.lists, block)
+
+        def core_sum(channel, held):
+            parts = [(arrived[channel][k], heads[k], room.far, 1, False) for k in range(half, vols)]
+            if room.pool:
+                parts.append((pools[channel], pools[0], room.pool, half, True))
+            keep, give = collect(parts, held, True, scalars, room.lists, block)
+            return keep + lax.ppermute(give, "pix", pairs)
 
         def pix_sum(mine):
             step = 2
@@ -391,20 +461,23 @@
                 step *= 2
             return mine
 
-        mine0 = core_sum(near0, far0, None)
-        mine0, near1[0] = lax.optimization_barrier((mine0, near1[0]))
-        held1 = collect(near1, None, None, cap, block)
+        mine0 = core_sum(0, near(0))
+        mine0, arrived[1][0] = lax.optimization_barrier((mine0, arrived[1][0]))
+        held1 = near(1)
         mine0 = pix_sum(mine0)
+        mine0, arrived[1][half] = lax.optimization_barrier((mine0, arrived[1][half]))
         result = finish(0, core, names, mine0, lax.ppermute(mine0, "pix", pairs), ())
-        far1[0], *result = lax.optimization_barrier((far1[0], *result))
-        mine1 = pix_sum(core_sum(near1, far1, held1))
+        mine1 = pix_sum(core_sum(1, held1))
         result = finish(1, core, names, mine1, lax.ppermute(mine1, "pix", pairs), result)
         return mine0[block // 2, 0] > 0, *result
 
-    result = exchange(most_rows * 23 // 32 // 8 * 8)
+    def rows_of(share):
+        return most_rows * share // 32 // 8 * 8
+
+    result = exchange(Room(vols, rows_of(23), rows_of(17), rows_of(6)))
 
     def redo(state):
-        unused, *full = exchange(most_rows)
+        unused, *full = exchange(Room(vols, most_rows, most_rows, 0))
         return jnp.zeros((), bool), *full
 
     _, owned, shell = lax.while_loop(lambda state: state[0], redo, result)

time: 78.5 us -> 82.6 us (1.052); the launches traced: 77.1 us -> 82.4 us
  starting transfers between devices: 30.6 us -> 37.8 us
  waiting for transfers between devices: 26.7 us -> 21.2 us
  Pallas kernels: 16.4 us -> 19.8 us
    ppermute x16 -> x22, starting transfers between devices: 27.3 us -> 35.2 us  [the longest x20 35.1 us: send(): return lax.ppermute(x, 'vol', [(d, d ^ k) for d in range(vols)])]
    ppermute x2, waiting for transfers between devices: 13.9 us -> 7.52 us  [pix_sum(): lax.ppermute(mine, 'pix', [(p, p ^ step) for p in range(pixs)])]
    pallas_call x7, Pallas kernels: 13.4 us -> 16.8 us  [the longest x2 8.91 us: project(): pl.pallas_call(functools.partial(project_kernel, steps, room, named), in_...]
    ppermute x16 -> x22, waiting for transfers between devices: 12.5 us -> 13.6 us  [the longest x20 12.1 us: send(): return lax.ppermute(x, 'vol', [(d, d ^ k) for d in range(vols)])]
  transfers between devices with their start and end apart: 20 -> 26, of which waited for: 9 -> 10; matrix products, arithmetic and copies ran while one was open for 1% -> 1% of each run, Pallas kernels for 10% -> 10%
where the time goes in v1:
time: 82.6 us; the launch traced here: 82.4 us
  starting transfers between devices  37.8 us (46%)
  waiting for transfers between devices  21.2 us (26%)
  Pallas kernels  19.8 us (24%)
  between operations  1.69 us (2%)
  local copies, waits for them, and re-layouts  1.68 us (2%)
    ppermute x20, starting transfers between devices, send(): return lax.ppermute(x, 'vol', [(d, d ^ k) for d in range(vols)])  35.1 us
    ppermute x20, waiting for transfers between devices, send(): return lax.ppermute(x, 'vol', [(d, d ^ k) for d in range(vols)])  12.1 us
    pallas_call x2, Pallas kernels, project(): pl.pallas_call(functools.partial(project_kernel, steps, room, named), in_...  8.91 us
    ppermute x2, waiting for transfers between devices, pix_sum(): lax.ppermute(mine, 'pix', [(p, p ^ step) for p in range(pixs)])  7.52 us
    pallas_call x4, Pallas kernels, collect(): pl.pallas_call(functools.partial(collect_kernel, tuple(items), lists, hel...  6.08 us
    ppermute x2, starting transfers between devices, pix_sum(): lax.ppermute(mine, 'pix', [(p, p ^ step) for p in range(pixs)])  2.53 us
    pallas_call x2, Pallas kernels, finish(): pl.pallas_call(functools.partial(finish_kernel, channel), in_specs=[SMEM,...  2.39 us
    pallas_call x1, Pallas kernels, plan(): pl.pallas_call(functools.partial(plan_kernel, room, block), in_specs=[SME...  1.82 us
  transfers between devices with their start and end apart: 26, of which 10 were waited for; matrix products, arithmetic and copies ran while one was open for 1% of the time, Pallas kernels for 10%

profile of v1, /device:TPU:0, one launch (start us, length us, event | category | flops | bytes accessed | tf_op | source)
XLA Modules:
  0.0 82.4 jit_solution(6900261175942770814)
XLA Ops:
  0.7 1.8 %plan.3 = (s32[8,128]{1,0:T(8,128)S(1)}, s32[8,128]{1,0:T(8,128)S(1)}, f32[72,128]{1,0:T(8,128)S(1)}) custom-call(s32[1]{0:T(128)} %bitcast.3.me_ref, s32[8,128]{1,0:T(8,128)} %bitcast.37, s32[128,128]{1,0:T(8,128)} %bitcast.26), custom_call_target="tpu_custom_call" | custom-call | tf_op jit(solution)/shard_map/plan/pallas_call | solution.py:128
  2.5 4.6 %project.6 = (f32[192,128]{1,0:T(8,128)S(1)}, f32[192,128]{1,0:T(8,128)S(1)}, f32[192,128]{1,0:T(8,128)S(1)}, f32[192,128]{1,0:T(8,128)S(1)}, f32[144,128]{1,0:T...) custom-call(s32[1024]{0:T(1024)S(1)} %bitcast.24, ...), custom_call_target="tpu_custom_call" | custom-call | tf_op jit(solution)/shard_map/project/pallas_call | solution.py:219
  7.1 4.1 %collective-permute-start.24 = (f32[56,128]{1,0:T(8,128)S(1)}, f32[56,128]{1,0:T(8,128)S(1)}, u32[]{:S(2)}, u32[]{:S(2)}) collective-permute-start(f32[56,128]{1,0:T(8,128)S(1)} %get-tuple-element.170), channel_id=1, source_target_pairs={{0,16},{4,20},{8,24},{12,28},{16,0},{20,4},{24,8},{28,12},{1,17},{... | collective-permute-start | bytes 86024 | tf_op jit(solution)/shard_map/ppermute | solution.py:411
  11.2 1.5 %collective-permute-start.27 = (f32[192,128]{1,0:T(8,128)S(1)}, f32[192,128]{1,0:T(8,128)S(1)}, u32[]{:S(2)}, u32[]{:S(2)}) collective-permute-start(f32[192,128]{1,0:T(8,128)S(1)} %get-tuple-element.173), channel_id=1, source_target_pairs={{0,4},{4,0},{8,12},{12,8},{16,20},{20,16},{24,28},{28,24},{1,5},{5... | collective-permute-start | bytes 294920 | tf_op jit(solution)/shard_map/ppermute | solution.py:411
  12.7 1.6 %collective-permute-start.28 = (f32[192,128]{1,0:T(8,128)S(1)}, f32[192,128]{1,0:T(8,128)S(1)}, u32[]{:S(2)}, u32[]{:S(2)}) collective-permute-start(f32[192,128]{1,0:T(8,128)S(1)} %get-tuple-element.174), channel_id=1, source_target_pairs={{0,8},{4,12},{8,0},{12,4},{16,24},{20,28},{24,16},{28,20},{1,9},{5... | collective-permute-start | bytes 294920 | tf_op jit(solution)/shard_map/ppermute | solution.py:411
  15.4 4.3 %project.7 = (f32[184,128]{1,0:T(8,128)S(1)}, f32[184,128]{1,0:T(8,128)S(1)}, f32[184,128]{1,0:T(8,128)S(1)}, f32[184,128]{1,0:T(8,128)S(1)}, f32[136,128]{1,0:T...) custom-call(s32[1024]{0:T(1024)S(1)} %bitcast.25, ...), custom_call_target="tpu_custom_call" | custom-call | tf_op jit(solution)/shard_map/project/pallas_call | solution.py:219
  19.8 1.6 %collective-permute-start.25 = (f32[56,128]{1,0:T(8,128)S(1)}, f32[56,128]{1,0:T(8,128)S(1)}, u32[]{:S(2)}, u32[]{:S(2)}) collective-permute-start(f32[56,128]{1,0:T(8,128)S(1)} %collective-permute-done.24), channel_id=1, source_target_pairs={{0,8},{4,12},{8,0},{12,4},{16,24},{20,28},{24,16},{28,20},{1,9},{5... | collective-permute-start | bytes 86024 | tf_op jit(solution)/shard_map/ppermute | solution.py:411
  21.4 2.3 %collective-permute-done.25 = f32[56,128]{1,0:T(8,128)S(1)} collective-permute-done((f32[56,128]{1,0:T(8,128)S(1)}, f32[56,128]{1,0:T(8,128)S(1)}, u32[]{:S(2)}, u32[]{:S(2)}) %collective-permute-start.25) | collective-permute-done | bytes 28704 | tf_op jit(solution)/shard_map/ppermute | solution.py:411
  23.7 1.5 %collective-permute-start.26 = (f32[112,128]{1,0:T(8,128)S(1)}, f32[112,128]{1,0:T(8,128)S(1)}, u32[]{:S(2)}, u32[]{:S(2)}) collective-permute-start(f32[112,128]{1,0:T(8,128)S(1)} %pad_maximum_fusion.1), channel_id=1, source_target_pairs={{0,4},{4,0},{8,12},{12,8},{16,20},{20,16},{24,28},{28,24},{1,5},{5... | collective-permute-start | bytes 172040 | tf_op jit(solution)/shard_map/ppermute | solution.py:411
  25.6 2.5 %collective-permute-start.21 = (f32[144,128]{1,0:T(8,128)S(1)}, f32[144,128]{1,0:T(8,128)S(1)}, u32[]{:S(2)}, u32[]{:S(2)}) collective-permute-start(f32[144,128]{1,0:T(8,128)S(1)} %get-tuple-element.155), channel_id=1, source_target_pairs={{0,20},{4,16},{8,28},{12,24},{16,4},{20,0},{24,12},{28,8},{1,21},{... | collective-permute-start | bytes 221192 | tf_op jit(solution)/shard_map/ppermute | solution.py:411
  30.8 3.4 %collective-permute-start.23 = (f32[144,128]{1,0:T(8,128)S(1)}, f32[144,128]{1,0:T(8,128)S(1)}, u32[]{:S(2)}, u32[]{:S(2)}) collective-permute-start(f32[144,128]{1,0:T(8,128)S(1)} %get-tuple-element.157), channel_id=1, source_target_pairs={{0,28},{4,24},{8,20},{12,16},{16,12},{20,8},{24,4},{28,0},{1,29},{... | collective-permute-start | bytes 221192 | tf_op jit(solution)/shard_map/ppermute | solution.py:411
  34.9 1.7 %collective-permute-done.21.refs_1_.refs_3_ = f32[144,128]{1,0:T(8,128)S(1)} collective-permute-done((f32[144,128]{1,0:T(8,128)S(1)}, f32[144,128]{1,0:T(8,128)S(1)}, u32[]{:S(2)}, u32[]{:S(2)}) %collective-permute-start.21) | collective-permute-done | bytes 73760 | tf_op jit(solution)/shard_map/ppermute | solution.py:411
  38.0 1.8 %collect_last.6 = (f32[520,128]{1,0:T(8,128)S(1)}, f32[520,128]{1,0:T(8,128)S(1)}) custom-call(s32[2]{0:T(128)S(1)} %pad_add_fusion.scalars_ref, f32[144,128]{1,0:T(8,128)S(1)} %collective-permute-done.20.refs_0_.refs_1_, f32[144,128]{1,0:T(8,128)S(1)} %collective-permute-done.21.refs_1_.refs_3_, f32[144,128]{1,0:T(8,128)S(1)} %collective-permute-done.22.refs_2_.refs_5_, ...), custom_call_target="tpu_custom_call" | custom-call | tf_op jit(solution)/shard_map/collect_last/pallas_call | solution.py:300
  39.9 2.7 %collective-permute-start.36 = (f32[48,128]{1,0:T(8,128)S(1)}, f32[48,128]{1,0:T(8,128)S(1)}, u32[]{:S(2)}, u32[]{:S(2)}) collective-permute-start(f32[48,128]{1,0:T(8,128)S(1)} %get-tuple-element.187), channel_id=1, source_target_pairs={{0,16},{4,20},{8,24},{12,28},{16,0},{20,4},{24,8},{28,12},{1,17},{... | collective-permute-start | bytes 73736 | tf_op jit(solution)/shard_map/ppermute | solution.py:411
  42.6 2.1 %collective-permute-done.36 = f32[48,128]{1,0:T(8,128)S(1)} collective-permute-done((f32[48,128]{1,0:T(8,128)S(1)}, f32[48,128]{1,0:T(8,128)S(1)}, u32[]{:S(2)}, u32[]{:S(2)}) %collective-permute-start.36) | collective-permute-done | bytes 24608 | tf_op jit(solution)/shard_map/ppermute | solution.py:411
  49.7 1.6 %collective-permute-start.31 = (f32[520,128]{1,0:T(8,128)S(1)}, f32[520,128]{1,0:T(8,128)S(1)}, u32[]{:S(2)}, u32[]{:S(2)}) collective-permute-start(f32[520,128]{1,0:T(8,128)S(1)} %add.28), channel_id=1, source_target_pairs={{0,2},{1,3},{2,0},{3,1},{4,6},{5,7},{6,4},{7,5},{8,10},{9,11},{10,... | collective-permute-start | bytes 798728 | tf_op jit(solution)/shard_map/ppermute | solution.py:460
  52.5 2.1 %collective-permute-start.32 = (f32[136,128]{1,0:T(8,128)S(1)}, f32[136,128]{1,0:T(8,128)S(1)}, u32[]{:S(2)}, u32[]{:S(2)}) collective-permute-start(f32[136,128]{1,0:T(8,128)S(1)} %get-tuple-element.180), channel_id=1, source_target_pairs={{0,16},{4,20},{8,24},{12,28},{16,0},{20,4},{24,8},{28,12},{1,17},{... | collective-permute-start | bytes 208904 | tf_op jit(solution)/shard_map/ppermute | solution.py:411
  55.7 2.6 %collective-permute-start.34 = (f32[136,128]{1,0:T(8,128)S(1)}, f32[136,128]{1,0:T(8,128)S(1)}, u32[]{:S(2)}, u32[]{:S(2)}) collective-permute-start(f32[136,128]{1,0:T(8,128)S(1)} %get-tuple-element.185), channel_id=1, source_target_pairs={{0,24},{4,28},{8,16},{12,20},{16,8},{20,12},{24,0},{28,4},{1,25},{... | collective-permute-start | bytes 208904 | tf_op jit(solution)/shard_map/ppermute | solution.py:411
  58.3 1.9 %collective-permute-start.35 = (f32[136,128]{1,0:T(8,128)S(1)}, f32[136,128]{1,0:T(8,128)S(1)}, u32[]{:S(2)}, u32[]{:S(2)}) collective-permute-start(f32[136,128]{1,0:T(8,128)S(1)} %get-tuple-element.186), channel_id=1, source_target_pairs={{0,28},{4,24},{8,20},{12,16},{16,12},{20,8},{24,4},{28,0},{1,29},{... | collective-permute-start | bytes 208904 | tf_op jit(solution)/shard_map/ppermute | solution.py:411
  62.3 1.7 %collective-permute-done.33.refs_2_ = f32[136,128]{1,0:T(8,128)S(1)} collective-permute-done((f32[136,128]{1,0:T(8,128)S(1)}, f32[136,128]{1,0:T(8,128)S(1)}, u32[]{:S(2)}, u32[]{:S(2)}) %collective-permute-start.33) | collective-permute-done | bytes 69664 | tf_op jit(solution)/shard_map/ppermute | solution.py:411
  63.9 1.5 %collective-permute-done.35.refs_6_ = f32[136,128]{1,0:T(8,128)S(1)} collective-permute-done((f32[136,128]{1,0:T(8,128)S(1)}, f32[136,128]{1,0:T(8,128)S(1)}, u32[]{:S(2)}, u32[]{:S(2)}) %collective-permute-start.35) | collective-permute-done | bytes 69664 | tf_op jit(solution)/shard_map/ppermute | solution.py:411
  65.4 1.8 %collect_last.7 = (f32[520,128]{1,0:T(8,128)S(1)}, f32[520,128]{1,0:T(8,128)S(1)}) custom-call(s32[2]{0:T(128)S(1)} %pad_add_fusion.scalars_ref, f32[136,128]{1,0:T(8,128)S(1)} %collective-permute-done.32.refs_0_, f32[144,128]{1,0:T(8,128)S(1)} %collective-permute-done.20.refs_0_.refs_1_, f32[136,128]{1,0:T(8,128)S(1)} %collective-permute-done.33.refs_2_, ...), custom_call_target="tpu_custom_call" | custom-call | tf_op jit(solution)/shard_map/collect_last/pallas_call | solution.py:300
  67.3 1.5 %collective-permute-done.42 = f32[520,128]{1,0:T(8,128)S(1)} collective-permute-done((f32[520,128]{1,0:T(8,128)S(1)}, f32[520,128]{1,0:T(8,128)S(1)}, u32[]{:S(2)}, u32[]{:S(2)}) %collective-permute-start.42) | collective-permute-done | bytes 266272 | tf_op jit(solution)/shard_map/ppermute | solution.py:455
  69.9 7.5 %collective-permute-done.43 = f32[520,128]{1,0:T(8,128)S(1)} collective-permute-done((f32[520,128]{1,0:T(8,128)S(1)}, f32[520,128]{1,0:T(8,128)S(1)}, u32[]{:S(2)}, u32[]{:S(2)}) %collective-permute-start.43) | collective-permute-done | bytes 266272 | tf_op jit(solution)/shard_map/ppermute | solution.py:460
  (67 shorter events, 21.0 us)
Async XLA Ops:
  7.1 12.7 %collective-permute-start.24 = (f32[56,128]{1,0:T(8,128)S(1)}, f32[56,128]{1,0:T(8,128)S(1)}, u32[]{:S(2)}, u32[]{:S(2)}) collective-permute-start(f32[56,128]{1,0:T(8,128)S(1)} %get-tuple-element.170), channel_id=1, source_target_pairs={{0,16},{4,20},{8,24},{12,28},{16,0},{20,4},{24,8},{28,12},{1,17},{... | collective-permute-start | bytes 86024 | tf_op jit(solution)/shard_map/ppermute | solution.py:411
  11.2 14.4 %collective-permute-start.27 = (f32[192,128]{1,0:T(8,128)S(1)}, f32[192,128]{1,0:T(8,128)S(1)}, u32[]{:S(2)}, u32[]{:S(2)}) collective-permute-start(f32[192,128]{1,0:T(8,128)S(1)} %get-tuple-element.173), channel_id=1, source_target_pairs={{0,4},{4,0},{8,12},{12,8},{16,20},{20,16},{24,28},{28,24},{1,5},{5... | collective-permute-start | bytes 294920 | tf_op jit(solution)/shard_map/ppermute | solution.py:411
  12.7 15.4 %collective-permute-start.28 = (f32[192,128]{1,0:T(8,128)S(1)}, f32[192,128]{1,0:T(8,128)S(1)}, u32[]{:S(2)}, u32[]{:S(2)}) collective-permute-start(f32[192,128]{1,0:T(8,128)S(1)} %get-tuple-element.174), channel_id=1, source_target_pairs={{0,8},{4,12},{8,0},{12,4},{16,24},{20,28},{24,16},{28,20},{1,9},{5... | collective-permute-start | bytes 294920 | tf_op jit(solution)/shard_map/ppermute | solution.py:411
  14.3 15.3 %collective-permute-start.29 = (f32[192,128]{1,0:T(8,128)S(1)}, f32[192,128]{1,0:T(8,128)S(1)}, u32[]{:S(2)}, u32[]{:S(2)}) collective-permute-start(f32[192,128]{1,0:T(8,128)S(1)} %get-tuple-element.175), channel_id=1, source_target_pairs={{0,12},{4,8},{8,4},{12,0},{16,28},{20,24},{24,20},{28,16},{1,13},{... | collective-permute-start | bytes 294920 | tf_op jit(solution)/shard_map/ppermute | solution.py:411
  19.8 3.9 %collective-permute-start.25 = (f32[56,128]{1,0:T(8,128)S(1)}, f32[56,128]{1,0:T(8,128)S(1)}, u32[]{:S(2)}, u32[]{:S(2)}) collective-permute-start(f32[56,128]{1,0:T(8,128)S(1)} %collective-permute-done.24), channel_id=1, source_target_pairs={{0,8},{4,12},{8,0},{12,4},{16,24},{20,28},{24,16},{28,20},{1,9},{5... | collective-permute-start | bytes 86024 | tf_op jit(solution)/shard_map/ppermute | solution.py:411
  23.7 10.5 %collective-permute-start.26 = (f32[112,128]{1,0:T(8,128)S(1)}, f32[112,128]{1,0:T(8,128)S(1)}, u32[]{:S(2)}, u32[]{:S(2)}) collective-permute-start(f32[112,128]{1,0:T(8,128)S(1)} %pad_maximum_fusion.1), channel_id=1, source_target_pairs={{0,4},{4,0},{8,12},{12,8},{16,20},{20,16},{24,28},{28,24},{1,5},{5... | collective-permute-start | bytes 172040 | tf_op jit(solution)/shard_map/ppermute | solution.py:411
  25.3 9.6 %collective-permute-start.20 = (f32[144,128]{1,0:T(8,128)S(1)}, f32[144,128]{1,0:T(8,128)S(1)}, u32[]{:S(2)}, u32[]{:S(2)}) collective-permute-start(f32[144,128]{1,0:T(8,128)S(1)} %get-tuple-element.154), channel_id=1, source_target_pairs={{0,16},{4,20},{8,24},{12,28},{16,0},{20,4},{24,8},{28,12},{1,17},{... | collective-permute-start | bytes 221192 | tf_op jit(solution)/shard_map/ppermute | solution.py:411
  25.6 10.9 %collective-permute-start.21 = (f32[144,128]{1,0:T(8,128)S(1)}, f32[144,128]{1,0:T(8,128)S(1)}, u32[]{:S(2)}, u32[]{:S(2)}) collective-permute-start(f32[144,128]{1,0:T(8,128)S(1)} %get-tuple-element.155), channel_id=1, source_target_pairs={{0,20},{4,16},{8,28},{12,24},{16,4},{20,0},{24,12},{28,8},{1,21},{... | collective-permute-start | bytes 221192 | tf_op jit(solution)/shard_map/ppermute | solution.py:411
  28.1 8.4 %collective-permute-start.22 = (f32[144,128]{1,0:T(8,128)S(1)}, f32[144,128]{1,0:T(8,128)S(1)}, u32[]{:S(2)}, u32[]{:S(2)}) collective-permute-start(f32[144,128]{1,0:T(8,128)S(1)} %get-tuple-element.156), channel_id=1, source_target_pairs={{0,24},{4,28},{8,16},{12,20},{16,8},{20,12},{24,0},{28,4},{1,25},{... | collective-permute-start | bytes 221192 | tf_op jit(solution)/shard_map/ppermute | solution.py:411
  30.8 7.2 %collective-permute-start.23 = (f32[144,128]{1,0:T(8,128)S(1)}, f32[144,128]{1,0:T(8,128)S(1)}, u32[]{:S(2)}, u32[]{:S(2)}) collective-permute-start(f32[144,128]{1,0:T(8,128)S(1)} %get-tuple-element.157), channel_id=1, source_target_pairs={{0,28},{4,24},{8,20},{12,16},{16,12},{20,8},{24,4},{28,0},{1,29},{... | collective-permute-start | bytes 221192 | tf_op jit(solution)/shard_map/ppermute | solution.py:411
  39.8 9.8 %collective-permute-start.30 = (f32[520,128]{1,0:T(8,128)S(1)}, f32[520,128]{1,0:T(8,128)S(1)}, u32[]{:S(2)}, u32[]{:S(2)}) collective-permute-start(f32[520,128]{1,0:T(8,128)S(1)} %get-tuple-element.177), channel_id=1, source_target_pairs={{0,1},{1,0},{2,3},{3,2},{4,5},{5,4},{6,7},{7,6},{8,9},{9,8},{10,11... | collective-permute-start | bytes 798728 | tf_op jit(solution)/shard_map/ppermute | solution.py:455
  39.9 4.8 %collective-permute-start.36 = (f32[48,128]{1,0:T(8,128)S(1)}, f32[48,128]{1,0:T(8,128)S(1)}, u32[]{:S(2)}, u32[]{:S(2)}) collective-permute-start(f32[48,128]{1,0:T(8,128)S(1)} %get-tuple-element.187), channel_id=1, source_target_pairs={{0,16},{4,20},{8,24},{12,28},{16,0},{20,4},{24,8},{28,12},{1,17},{... | collective-permute-start | bytes 73736 | tf_op jit(solution)/shard_map/ppermute | solution.py:411
  44.7 6.5 %collective-permute-start.37 = (f32[48,128]{1,0:T(8,128)S(1)}, f32[48,128]{1,0:T(8,128)S(1)}, u32[]{:S(2)}, u32[]{:S(2)}) collective-permute-start(f32[48,128]{1,0:T(8,128)S(1)} %collective-permute-done.36), channel_id=1, source_target_pairs={{0,8},{4,12},{8,0},{12,4},{16,24},{20,28},{24,16},{28,20},{1,9},{5... | collective-permute-start | bytes 73736 | tf_op jit(solution)/shard_map/ppermute | solution.py:411
  46.1 6.4 %collective-permute-start.39 = (f32[184,128]{1,0:T(8,128)S(1)}, f32[184,128]{1,0:T(8,128)S(1)}, u32[]{:S(2)}, u32[]{:S(2)}) collective-permute-start(f32[184,128]{1,0:T(8,128)S(1)} %get-tuple-element.189), channel_id=1, source_target_pairs={{0,4},{4,0},{8,12},{12,8},{16,20},{20,16},{24,28},{28,24},{1,5},{5... | collective-permute-start | bytes 282632 | tf_op jit(solution)/shard_map/ppermute | solution.py:411
  47.4 7.2 %collective-permute-start.40 = (f32[184,128]{1,0:T(8,128)S(1)}, f32[184,128]{1,0:T(8,128)S(1)}, u32[]{:S(2)}, u32[]{:S(2)}) collective-permute-start(f32[184,128]{1,0:T(8,128)S(1)} %get-tuple-element.190), channel_id=1, source_target_pairs={{0,8},{4,12},{8,0},{12,4},{16,24},{20,28},{24,16},{28,20},{1,9},{5... | collective-permute-start | bytes 282632 | tf_op jit(solution)/shard_map/ppermute | solution.py:411
  48.5 7.2 %collective-permute-start.41 = (f32[184,128]{1,0:T(8,128)S(1)}, f32[184,128]{1,0:T(8,128)S(1)}, u32[]{:S(2)}, u32[]{:S(2)}) collective-permute-start(f32[184,128]{1,0:T(8,128)S(1)} %get-tuple-element.191), channel_id=1, source_target_pairs={{0,12},{4,8},{8,4},{12,0},{16,28},{20,24},{24,20},{28,16},{1,13},{... | collective-permute-start | bytes 282632 | tf_op jit(solution)/shard_map/ppermute | solution.py:411
  49.7 11.8 %collective-permute-start.31 = (f32[520,128]{1,0:T(8,128)S(1)}, f32[520,128]{1,0:T(8,128)S(1)}, u32[]{:S(2)}, u32[]{:S(2)}) collective-permute-start(f32[520,128]{1,0:T(8,128)S(1)} %add.28), channel_id=1, source_target_pairs={{0,2},{1,3},{2,0},{3,1},{4,6},{5,7},{6,4},{7,5},{8,10},{9,11},{10,... | collective-permute-start | bytes 798728 | tf_op jit(solution)/shard_map/ppermute | solution.py:460
  51.2 7.1 %collective-permute-start.38 = (f32[96,128]{1,0:T(8,128)S(1)}, f32[96,128]{1,0:T(8,128)S(1)}, u32[]{:S(2)}, u32[]{:S(2)}) collective-permute-start(f32[96,128]{1,0:T(8,128)S(1)} %pad_maximum_fusion.2), channel_id=1, source_target_pairs={{0,4},{4,0},{8,12},{12,8},{16,20},{20,16},{24,28},{28,24},{1,5},{5... | collective-permute-start | bytes 147464 | tf_op jit(solution)/shard_map/ppermute | solution.py:411
  52.5 9.7 %collective-permute-start.32 = (f32[136,128]{1,0:T(8,128)S(1)}, f32[136,128]{1,0:T(8,128)S(1)}, u32[]{:S(2)}, u32[]{:S(2)}) collective-permute-start(f32[136,128]{1,0:T(8,128)S(1)} %get-tuple-element.180), channel_id=1, source_target_pairs={{0,16},{4,20},{8,24},{12,28},{16,0},{20,4},{24,8},{28,12},{1,17},{... | collective-permute-start | bytes 208904 | tf_op jit(solution)/shard_map/ppermute | solution.py:411
  54.6 9.3 %collective-permute-start.33 = (f32[136,128]{1,0:T(8,128)S(1)}, f32[136,128]{1,0:T(8,128)S(1)}, u32[]{:S(2)}, u32[]{:S(2)}) collective-permute-start(f32[136,128]{1,0:T(8,128)S(1)} %get-tuple-element.184), channel_id=1, source_target_pairs={{0,20},{4,16},{8,28},{12,24},{16,4},{20,0},{24,12},{28,8},{1,21},{... | collective-permute-start | bytes 208904 | tf_op jit(solution)/shard_map/ppermute | solution.py:411
  55.7 8.2 %collective-permute-start.34 = (f32[136,128]{1,0:T(8,128)S(1)}, f32[136,128]{1,0:T(8,128)S(1)}, u32[]{:S(2)}, u32[]{:S(2)}) collective-permute-start(f32[136,128]{1,0:T(8,128)S(1)} %get-tuple-element.185), channel_id=1, source_target_pairs={{0,24},{4,28},{8,16},{12,20},{16,8},{20,12},{24,0},{28,4},{1,25},{... | collective-permute-start | bytes 208904 | tf_op jit(solution)/shard_map/ppermute | solution.py:411
  58.3 7.1 %collective-permute-start.35 = (f32[136,128]{1,0:T(8,128)S(1)}, f32[136,128]{1,0:T(8,128)S(1)}, u32[]{:S(2)}, u32[]{:S(2)}) collective-permute-start(f32[136,128]{1,0:T(8,128)S(1)} %get-tuple-element.186), channel_id=1, source_target_pairs={{0,28},{4,24},{8,20},{12,16},{16,12},{20,8},{24,4},{28,0},{1,29},{... | collective-permute-start | bytes 208904 | tf_op jit(solution)/shard_map/ppermute | solution.py:411
  68.9 8.5 %collective-permute-start.43 = (f32[520,128]{1,0:T(8,128)S(1)}, f32[520,128]{1,0:T(8,128)S(1)}, u32[]{:S(2)}, u32[]{:S(2)}) collective-permute-start(f32[520,128]{1,0:T(8,128)S(1)} %add.30), channel_id=1, source_target_pairs={{0,2},{1,3},{2,0},{3,1},{4,6},{5,7},{6,4},{7,5},{8,10},{9,11},{10,... | collective-permute-start | bytes 798728 | tf_op jit(solution)/shard_map/ppermute | solution.py:460
  69.9 8.8 %collective-permute-start.45 = (f32[520,128]{1,0:T(8,128)S(1)}, f32[520,128]{1,0:T(8,128)S(1)}, u32[]{:S(2)}, u32[]{:S(2)}) collective-permute-start(f32[520,128]{1,0:T(8,128)S(1)} %add.29.mine_ref), channel_id=1, source_target_pairs={{0,1},{1,0},{2,3},{3,2},{4,5},{5,4},{6,7},{7,6},{8,9},{9,8},{10,11... | collective-permute-start | bytes 798728 | tf_op jit(solution)/shard_map/ppermute | solution.py:469
  (9 other events, 115.0 us)

commit v2 on v0

v2 whole, which is shorter than its diff:
```python
import functools

import jax
import jax.numpy as jnp
from jax import lax
from jax.experimental import pallas as pl
from jax.experimental.pallas import tpu as pltpu
from jax.sharding import PartitionSpec as P


LANES = 128
HEAD = 8
ROOM = pltpu.CompilerParams(vmem_limit_bytes=16 << 20)
GROUP = 256
WINDOW = 40


SMEM = pl.BlockSpec(memory_space=pltpu.SMEM)
VMEM = pl.BlockSpec(memory_space=pltpu.VMEM)
ANY = pl.BlockSpec(memory_space=pl.ANY)
HBM = pl.BlockSpec(memory_space=pltpu.HBM)


def iota(shape, axis):
    return lax.broadcasted_iota(jnp.int32, shape, axis)


def nt_dot(a, b):
    return lax.dot_general(a, b, (((1,), (1,)), ((), ())), preferred_element_type=jnp.float32)


def dot(a, b):
    return jnp.dot(a, b, preferred_element_type=jnp.float32)


def ones_where(mask):
    return jnp.where(mask, 1.0, 0.0).astype(jnp.bfloat16)


def bytes_of(x):
    return (x >> 8).astype(jnp.float32), (x & 255).astype(jnp.float32)


def running_counts(marks, rows):
    total = marks.shape[0]
    upper = ones_where(iota((LANES, LANES), 0) <= iota((LANES, LANES), 1))
    row, column = iota((total, total), 0), iota((total, total), 1)
    earlier = ones_where((column < row) & (row // rows == column // rows))
    before = dot(earlier, marks).astype(jnp.bfloat16)
    return dot(marks, upper) + dot(before, jnp.ones((LANES, LANES), jnp.bfloat16))


def plan_kernel(vols, parts, block, cap, me_ref, tile_ref, slot_ref, place_ref, ends_ref, head_ref):
    size = cap + HEAD
    part_tiles = block // parts
    lane = iota((HEAD, LANES), 1)
    line = iota((HEAD, LANES), 0)
    slots = slot_ref[...]
    ends = ones_where(((line == 0) & (lane == 0)) | ((line == 1) & (lane == LANES - 1)))
    high, low = bytes_of(slots)
    ends_ref[...] = (
        nt_dot(ends, high.astype(jnp.bfloat16)) * 256.0 + nt_dot(ends, low.astype(jnp.bfloat16))
    ).astype(jnp.int32)

    tiles = tile_ref[...]
    rows = tiles.shape[0]
    classes = vols * parts
    part = tiles // part_tiles
    group = part ^ (me_ref[0] * parts + me_ref[1])
    marks = jnp.concatenate([jnp.where(group == i, 1.0, 0.0) for i in range(classes)], axis=0)
    counts = running_counts(marks.astype(jnp.bfloat16), rows) * marks
    place = jnp.zeros((rows, LANES), jnp.float32)
    for i in range(classes):
        place = place + counts[i * rows : (i + 1) * rows]
    place = place.astype(jnp.int32) - 1
    fits = place < cap
    place_ref[...] = jnp.where(fits, group * size + place, classes * size)
    spilled = jnp.sum(jnp.where(fits, 0.0, 1.0), axis=(0, 1), keepdims=True)
    lists = -(-2 * size // LANES)
    width = lists * LANES
    spot = jnp.where(fits, place + me_ref[2] * size, -1)
    high, low = bytes_of(tiles - part * part_tiles + 1)
    ids = jnp.zeros((2 * classes, width), jnp.float32)
    which = iota((classes, LANES), 0)
    for r in range(rows):
        here = group[r : r + 1] == which
        pieces = jnp.concatenate(
            [jnp.where(here, high[r : r + 1], 0.0), jnp.where(here, low[r : r + 1], 0.0)], axis=0
        )
        spots = ones_where(iota((width, LANES), 0) == spot[r : r + 1])
        ids = ids + nt_dot(pieces.astype(jnp.bfloat16), spots)
    ids = ids[:classes] * 256.0 + ids[classes:]
    for k in range(classes):
        head = jnp.where(line == lists, jnp.broadcast_to(spilled, (HEAD, LANES)), 0.0)
        for i in range(lists):
            head = jnp.where(line == i, ids[k : k + 1, i * LANES : (i + 1) * LANES], head)
        head_ref[k * HEAD : (k + 1) * HEAD, :] = head


def plan(me, tiles, slot, vols, parts, block, cap):
    rows = tiles.shape[0]
    return pl.pallas_call(
        functools.partial(plan_kernel, vols, parts, block, cap),
        in_specs=[SMEM, VMEM, VMEM],
        out_specs=[VMEM, VMEM, VMEM],
        out_shape=[
            jax.ShapeDtypeStruct((rows, LANES), jnp.int32),
            jax.ShapeDtypeStruct((HEAD, slot.shape[0]), jnp.int32),
            jax.ShapeDtypeStruct((vols * parts * HEAD, LANES), jnp.float32),
        ],
        compiler_params=ROOM,
        name="plan",
    )(me, tiles, slot)


def project_kernel(
    steps, cap, own, me_ref, ends_ref, place_ref, kernel_hbm, thermal_ref, kinetic_ref, slot_ref, head_ref,
    out_ref, kernel_ref, partial_ref, stage_ref, factor_s, in_sem
):
    entries, _ = kernel_ref.shape
    part = entries // steps
    groups = part // GROUP
    lines = GROUP // LANES
    slots = place_ref.shape[0]
    total = entries // LANES

    def load(step):
        piece = pl.ds(pl.multiple_of(step * part, part), part)
        return pltpu.make_async_copy(kernel_hbm.at[piece], kernel_ref.at[piece], in_sem.at[step])

    for step in range(steps):
        load(step).start()
    partial_ref[...] = jnp.zeros_like(partial_ref)
    stage_ref[...] = jnp.zeros_like(stage_ref)
    first_channel = (me_ref[2] == 0) == own
    factor_s[...] = jnp.where(first_channel, thermal_ref[...].astype(jnp.float32), kinetic_ref[...].astype(jnp.float32))
    line = iota((WINDOW, LANES), 0)

    def first(group):
        return ends_ref[group * lines] & -8

    def reach(group):
        return ends_ref[total + group * lines + lines - 1] - first(group)

    def add(group, base):
        row = []
        for r in range(lines):
            at = pl.ds(group * lines + r, 1)
            row.append(jnp.where(line == slot_ref[at, :] - base, factor_s[at, :], 0.0))
        weights = jnp.concatenate(row, axis=1).astype(jnp.bfloat16)
        sums = dot(weights, kernel_ref[pl.ds(pl.multiple_of(group * GROUP, GROUP), GROUP), :])
        partial_ref[pl.ds(pl.multiple_of(base, 8), WINDOW), :] += sums

    def turn(step, most):
        load(step).wait()
        for g in range(groups):
            group = step * groups + g
            add(group, first(group))
            most = jnp.maximum(most, reach(group))
        return most

    most = lax.fori_loop(0, steps, turn, 0)

    @pl.when(most >= WINDOW)
    def _():
        def more(group, carry):
            def again(w, inner):
                add(group, first(group) + w * WINDOW)
                return inner

            return lax.fori_loop(1, reach(group) // WINDOW + 1, again, carry)

        lax.fori_loop(0, steps * groups, more, 0)

    unroll = 16

    def move(i, carry):
        for u in range(unroll):
            s = i * unroll + u
            stage_ref[pl.ds(place_ref[s], 1), :] = partial_ref[pl.ds(s, 1), :]
        return carry

    lax.fori_loop(0, slots // unroll, move, 0)
    size = cap + HEAD
    for k in range(head_ref.shape[0] // HEAD):
        out_ref[k * size : k * size + cap, :] = stage_ref[k * size : k * size + cap, :]
        out_ref[k * size + cap : (k + 1) * size, :] = head_ref[k * HEAD : (k + 1) * HEAD, :]


def project(me, kernel, factors, slot, ends, place, head, cap, own):
    entries, pixels = kernel.shape
    slots = place.shape[0]
    steps = 4
    rows = head.shape[0] // HEAD * (cap + HEAD)
    return pl.pallas_call(
        functools.partial(project_kernel, steps, cap, own),
        in_specs=[SMEM, SMEM, SMEM, HBM, VMEM, VMEM, VMEM, VMEM],
        out_specs=VMEM,
        out_shape=jax.ShapeDtypeStruct((rows, pixels), jnp.float32),
        scratch_shapes=[
            pltpu.VMEM((entries, pixels), kernel.dtype),
            pltpu.VMEM((slots + WINDOW, pixels), jnp.float32),
            pltpu.VMEM((rows + HEAD, pixels), jnp.float32),
            pltpu.VMEM(slot.shape, jnp.float32),
            pltpu.SemaphoreType.DMA((steps,)),
        ],
        compiler_params=ROOM,
        name="project",
    )(me, ends, place, kernel, *factors, slot, head)


def pack_kernel(first, size, me_ref, mine_ref, other_ref, *outs):
    core = me_ref[2]
    for at, rows in ((core, mine_ref), (1 - core, other_ref)):
        at = pl.ds(pl.multiple_of(at * size, 8), size)
        for k, out in enumerate(outs):
            out[at, :] = rows[(first + k) * size : (first + k + 1) * size, :]


def pack(me, mine, other, first, count, size):
    out = jax.ShapeDtypeStruct((2 * size, mine.shape[1]), jnp.float32)
    return pl.pallas_call(
        functools.partial(pack_kernel, first, size),
        in_specs=[SMEM, VMEM, VMEM],
        out_specs=[VMEM] * count,
        out_shape=[out] * count,
        compiler_params=ROOM,
        name="pack",
    )(me, mine, other)


def split(x):
    high = x.astype(jnp.bfloat16)
    return high, (x - high.astype(jnp.float32)).astype(jnp.bfloat16)


def collect_kernel(size, part_tiles, *refs):
    messages, (out_ref, *rows_s) = refs[: len(refs) // 2], refs[len(refs) // 2 :]
    pixels = out_ref.shape[1]
    lists = -(-2 * size // LANES)
    flag = jnp.zeros((HEAD, pixels), jnp.float32)
    ids = []
    for message, rows in zip(messages, rows_s):
        rows[...] = jnp.concatenate(split(message[...]), axis=1)
        head = message[size - HEAD : size, :] + message[2 * size - HEAD : 2 * size, :]
        flag = flag + head[lists : lists + 1]
        names = jnp.concatenate([head[i : i + 1] for i in range(lists)], axis=1)[:, : 2 * size]
        ids.append(names.astype(jnp.int32) - 1)
    chunk = min(256, part_tiles)
    for t in range(0, part_tiles, chunk):
        sums = jnp.zeros((chunk, 2 * pixels), jnp.float32)
        for names, rows in zip(ids, rows_s):
            sums = sums + dot(ones_where(iota((chunk, 2 * size), 0) + t == names), rows[...])
        out_ref[t : t + chunk, :] = sums[:, :pixels] + sums[:, pixels:]
    out_ref[part_tiles:, :] = flag


def collect(messages, part_tiles):
    rows, pixels = messages[0].shape
    return pl.pallas_call(
        functools.partial(collect_kernel, rows // 2, part_tiles),
        in_specs=[VMEM] * len(messages),
        out_specs=VMEM,
        out_shape=jax.ShapeDtypeStruct((part_tiles + HEAD, pixels), jnp.float32),
        scratch_shapes=[pltpu.VMEM((rows, 2 * pixels), jnp.bfloat16)] * len(messages),
        compiler_params=ROOM,
        name="collect",
    )(*messages)


def owner_kernel(parts, me_ref, owner_ref, row_ref):
    most = row_ref.shape[1]
    owners = owner_ref[...]
    rows = owners.shape[0]
    mine = owners == me_ref[1] * 2 + me_ref[2]
    marks = jnp.where(mine, 1.0, 0.0)
    rank = running_counts(marks.astype(jnp.bfloat16), rows).astype(jnp.int32) - 1
    index = iota((rows, LANES), 0) * LANES + iota((rows, LANES), 1)
    found = jnp.zeros((HEAD, most), jnp.float32)
    line = iota((HEAD, LANES), 0)
    high, low = bytes_of(index + 1)
    for r in range(rows):
        pieces = jnp.where(line == 0, high[r : r + 1], jnp.where(line == 1, low[r : r + 1], 0.0))
        pieces = jnp.where(mine[r : r + 1], pieces, 0.0)
        spots = ones_where(iota((most, LANES), 0) == rank[r : r + 1])
        found = found + nt_dot(pieces.astype(jnp.bfloat16), spots)
    tile = (found[0:1] * 256.0 + found[1:2]).astype(jnp.int32) - 1
    tile = jnp.where(tile < 0, rows * LANES, tile)
    bounds = jnp.zeros((1, most), jnp.float32)
    for p in range(1, parts + 1):
        before = jnp.where(index < p * (rows * LANES // parts), marks, 0.0)
        bounds = jnp.where(iota((1, most), 1) == p, jnp.sum(before, axis=(0, 1), keepdims=True), bounds)
    row_ref[...] = jnp.where(iota((HEAD, most), 0) == 0, tile, bounds.astype(jnp.int32))


def owned_rows(me, owners, most, parts):
    return pl.pallas_call(
        functools.partial(owner_kernel, parts),
        in_specs=[SMEM, VMEM],
        out_specs=VMEM,
        out_shape=jax.ShapeDtypeStruct((HEAD, most), jnp.int32),
        compiler_params=ROOM,
        name="owned_rows",
    )(me, owners)


def fill_rows(row_ref, table_ref, owned_ref, start, end):
    unroll = 8

    def one(r):
        owned_ref[pl.ds(r, 1), :] = table_ref[pl.ds(row_ref[r], 1), :]

    def group(i, carry):
        for u in range(unroll):
            one(start + i * unroll + u)
        return carry

    def rest(r, carry):
        one(r)
        return carry

    groups = (end - start) // unroll
    lax.fori_loop(0, groups, group, 0)
    lax.fori_loop(start + groups * unroll, end, rest, 0)


def place_part(m, part_tiles, me_ref, own_ref, other_ref, map_ref):
    pixels = own_ref.shape[1]
    own, other = own_ref[:part_tiles, :], other_ref[:part_tiles, :]
    at = pl.ds(pl.multiple_of((me_ref[1] ^ m) * part_tiles, part_tiles), part_tiles)
    map_ref[at, :pixels] = jnp.where(me_ref[2] == 0, own, other)
    map_ref[at, pixels:] = jnp.where(me_ref[2] == 0, other, own)


def early_kernel(parts, me_ref, row_ref, own_ref, other_ref, owned_ref, map_ref):
    most = owned_ref.shape[0]
    owned_ref[...] = jnp.zeros_like(owned_ref)
    place_part(0, map_ref.shape[0] // parts, me_ref, own_ref, other_ref, map_ref)
    x = me_ref[1]
    fill_rows(row_ref, map_ref, owned_ref, row_ref[most + x], row_ref[most + x + 1])


def late_kernel(parts, me_ref, row_ref, *refs):
    pieces, (early_owned, early_map, owned_ref, map_ref) = refs[:-4], refs[-4:]
    most = owned_ref.shape[0]
    part_tiles = map_ref.shape[0] // parts
    x = me_ref[1]
    mine = pl.ds(pl.multiple_of(x * part_tiles, part_tiles), part_tiles)
    owned_ref[...] = early_owned[...]
    map_ref[mine, :] = early_map[mine, :]
    for m in range(1, parts):
        place_part(m, part_tiles, me_ref, pieces[2 * m - 2], pieces[2 * m - 1], map_ref)
    fill_rows(row_ref, map_ref, owned_ref, 0, row_ref[most + x])
    fill_rows(row_ref, map_ref, owned_ref, row_ref[most + x + 1], row_ref[most + parts])


def finish(kernel, me, rows, pieces, most, block, parts):
    width = 2 * pieces[0].shape[1]
    return pl.pallas_call(
        functools.partial(kernel, parts),
        in_specs=[SMEM, SMEM] + [VMEM] * len(pieces),
        out_specs=[VMEM, VMEM],
        out_shape=[
            jax.ShapeDtypeStruct((most, width), jnp.float32),
            jax.ShapeDtypeStruct((block, width), jnp.float32),
        ],
        compiler_params=ROOM,
    )(me, rows, *pieces)


def shards(kernel, pressure, velocity, entry_slot, slot_tile, tile_owner):
    vols = lax.axis_size("vol")
    pixs = lax.axis_size("pix")
    vol = lax.axis_index("vol")
    pix = lax.axis_index("pix")
    entries, _ = kernel.shape
    slots = slot_tile.shape[1]
    block = tile_owner.shape[0] // vols
    parts = pixs // 2
    part_tiles = block // parts
    half = vols // 2
    most_owned = 2 * block // pixs
    most_rows = min(2 * slots // vols, part_tiles)
    me = jnp.stack([vol, pix >> 1, pix & 1]).astype(jnp.int32)
    tiles = slot_tile.reshape(slots // LANES, LANES)
    slot = entry_slot.reshape(entries // LANES, LANES)
    factors = [x.reshape(entries // LANES, LANES) for x in (pressure, velocity)]
    owners = lax.dynamic_slice_in_dim(
        tile_owner.reshape(vols, block // LANES, LANES), vol, 1
    )[0]
    rows = owned_rows(me, owners, most_owned, parts)[:2].reshape(-1)

    def send(x, vol_step=0, part_step=0, core_step=0):
        step = (vol_step * parts + part_step) * 2 + core_step
        return lax.ppermute(x, ("vol", "pix"), [(d, d ^ step) for d in range(vols * pixs)])

    def exchange(cap):
        size = cap + HEAD
        count = half * parts
        place, ends, head = plan(me, tiles, slot, vols, parts, block, cap)
        place, ends = place.reshape(-1), ends.reshape(-1)
        given = project(me, kernel, factors, slot, ends, place, head, cap, False)
        taken = send(given, core_step=1)
        held = project(me, kernel, factors, slot, ends, place, head, cap, True)

        def gather(first):
            messages = list(pack(me, held, taken, first, count, size))
            for k in reversed(range(1, count)):
                messages[k] = send(messages[k], k // parts, k % parts)
            return collect(messages, part_tiles)

        far = send(gather(count), vol_step=half)
        mine = gather(0) + far
        other = send(mine, core_step=1)
        early = finish(early_kernel, me, rows, [mine, other], most_owned, block, parts)
        pieces = []
        for m in range(1, parts):
            piece = send(mine, part_step=m)
            pieces += [piece, send(piece, core_step=1)]
        full = finish(late_kernel, me, rows, [*pieces, *early], most_owned, block, parts)
        return mine[part_tiles, 0] > 0, *full

    result = exchange(most_rows * 13 // 32 // 8 * 8)

    def redo(state):
        unused, *full = exchange(most_rows)
        return jnp.zeros((), bool), *full

    _, owned, shell = lax.while_loop(lambda state: state[0], redo, result)
    return owned, shell


def solution(mesh):
    in_specs = (
        P(("vol", "pix"), None),
        P(("vol", "pix")),
        P(("vol", "pix")),
        P(("vol", "pix"), None),
        P(("vol", "pix"), None),
        P(),
    )
    out_specs = (P(("vol", "pix"), None), P("vol", None))
    return jax.shard_map(shards, mesh=mesh, in_specs=in_specs, out_specs=out_specs, check_vma=False)
```

time: 78.5 us -> 67.3 us (0.86)
  the two profiles are of different devices: /device:TPU:0 before, /device:TPU:1 now
where the time goes in v2:
time: 67.3 us; the launch traced here: 67.2 us
  starting transfers between devices  28.7 us (43%)
  Pallas kernels  18.3 us (27%)
  waiting for transfers between devices  17.9 us (27%)
  between operations  1.5 us (2%)
    ppermute x19, starting transfers between devices, send(): lax.ppermute(x, ('vol', 'pix'), [(d, d ^ step) for d in range(vols * pixs)])  28.7 us
    ppermute x19, waiting for transfers between devices, send(): lax.ppermute(x, ('vol', 'pix'), [(d, d ^ step) for d in range(vols * pixs)])  17.9 us
    pallas_call x2, Pallas kernels, project(): pl.pallas_call(functools.partial(project_kernel, steps, cap, own), in_spe...  8.49 us
    pallas_call x2, Pallas kernels, finish(): pl.pallas_call(functools.partial(kernel, parts), in_specs=[SMEM, SMEM] +...  4.42 us
    pallas_call x1, Pallas kernels, plan(): pl.pallas_call(functools.partial(plan_kernel, vols, parts, block, cap), i...  1.58 us
    pallas_call x2, Pallas kernels, collect(): pl.pallas_call(functools.partial(collect_kernel, rows // 2, part_tiles),...  1.46 us
  transfers between devices with their start and end apart: 19, of which 8 were waited for; matrix products, arithmetic and copies ran while one was open for 1% of the time, Pallas kernels for 11%

profile of v2, /device:TPU:1, one launch (start us, length us, event | category | flops | bytes accessed | tf_op | source)
XLA Modules:
  0.0 67.2 jit_solution(18056504941135616016)
XLA Ops:
  0.7 1.6 %plan.3 = (s32[8,128]{1,0:T(8,128)S(1)}, s32[8,128]{1,0:T(8,128)S(1)}, f32[128,128]{1,0:T(8,128)S(1)}) custom-call(s32[3]{0:T(128)S(1)} %pad_add_fusion.me_ref, s32[8,128]{1,0:T(8,128)} %bitcast.40, s32[128,128]{1,0:T(8,128)} %bitcast.27), custom_call_target="tpu_custom_call" | custom-call | tf_op jit(solution)/shard_map/plan/pallas_call | solution.py:102
  2.4 5.0 %project.7 = f32[1792,128]{1,0:T(8,128)S(1)} custom-call(s32[3]{0:T(128)S(1)} %pad_add_fusion.me_ref, s32[1024]{0:T(1024)S(1)} %bitcast.25, s32[1024]{0:T(1024)S(1)} %bitcast.23, bf16[16384,128]{1,0:T(8,128)(2,1)} %kernel_hbm.3, bf16[128,128]{1,0:T(8,128)(2,1)} %bitcast.31, bf16[128,128]{1,0:T(8,128)(2,1)} %bitcast.34, s32[128,128]{1,0:T(8,128)} %bitcast.28, ...), custom_call_target="tpu_custom_call" | custom-call | tf_op jit(solution)/shard_map/project/pallas_call | solution.py:195
  7.5 3.5 %project.6.mine_ref = f32[1792,128]{1,0:T(8,128)S(1)} custom-call(s32[3]{0:T(128)S(1)} %pad_add_fusion.me_ref, s32[1024]{0:T(1024)S(1)} %bitcast.26, s32[1024]{0:T(1024)S(1)} %bitcast.24, bf16[16384,128]{1,0:T(8,128)(2,1)S(1)} %copy-done.1, bf16[128,128]{1,0:T(8,128)(2,1)S(1)} %bitcast.32, bf16[128,128]{1,0:T(8,128)(2,1)S(1)} %bitcast.35, ...), custom_call_target="tpu_custom_call" | custom-call | tf_op jit(solution)/shard_map/project/pallas_call | solution.py:195
  11.6 2.7 %collective-permute-start.27 = (f32[224,128]{1,0:T(8,128)S(1)}, f32[224,128]{1,0:T(8,128)S(1)}, u32[]{:S(2)}, u32[]{:S(2)}) collective-permute-start(f32[224,128]{1,0:T(8,128)S(1)} %get-tuple-element.110), channel_id=1, source_target_pairs={{0,2},{1,3},{2,0},{3,1},{4,6},{5,7},{6,4},{7,5},{8,10},{9,11},{10,... | collective-permute-start | bytes 344072 | tf_op jit(solution)/shard_map/ppermute | solution.py:395
  14.3 1.2 %collective-permute-start.28 = (f32[224,128]{1,0:T(8,128)S(1)}, f32[224,128]{1,0:T(8,128)S(1)}, u32[]{:S(2)}, u32[]{:S(2)}) collective-permute-start(f32[224,128]{1,0:T(8,128)S(1)} %get-tuple-element.111), channel_id=1, source_target_pairs={{0,4},{1,5},{2,6},{3,7},{4,0},{5,1},{6,2},{7,3},{8,12},{9,13},{10,... | collective-permute-start | bytes 344072 | tf_op jit(solution)/shard_map/ppermute | solution.py:395
  15.6 1.5 %collective-permute-start.30 = (f32[224,128]{1,0:T(8,128)S(1)}, f32[224,128]{1,0:T(8,128)S(1)}, u32[]{:S(2)}, u32[]{:S(2)}) collective-permute-start(f32[224,128]{1,0:T(8,128)S(1)} %get-tuple-element.113), channel_id=1, source_target_pairs={{0,8},{1,9},{2,10},{3,11},{4,12},{5,13},{6,14},{7,15},{8,0},{9,1},... | collective-permute-start | bytes 344072 | tf_op jit(solution)/shard_map/ppermute | solution.py:395
  18.2 2.3 %collective-permute-start.32 = (f32[224,128]{1,0:T(8,128)S(1)}, f32[224,128]{1,0:T(8,128)S(1)}, u32[]{:S(2)}, u32[]{:S(2)}) collective-permute-start(f32[224,128]{1,0:T(8,128)S(1)} %get-tuple-element.115), channel_id=1, source_target_pairs={{0,12},{1,13},{2,14},{3,15},{4,8},{5,9},{6,10},{7,11},{8,4},{9,5},... | collective-permute-start | bytes 344072 | tf_op jit(solution)/shard_map/ppermute | solution.py:395
  21.1 1.7 %collective-permute-done.31.refs_5_ = f32[224,128]{1,0:T(8,128)S(1)} collective-permute-done((f32[224,128]{1,0:T(8,128)S(1)}, f32[224,128]{1,0:T(8,128)S(1)}, u32[]{:S(2)}, u32[]{:S(2)}) %collective-permute-start.31) | collective-permute-done | bytes 114720 | tf_op jit(solution)/shard_map/ppermute | solution.py:395
  22.8 2.8 %collective-permute-done.32.refs_6_ = f32[224,128]{1,0:T(8,128)S(1)} collective-permute-done((f32[224,128]{1,0:T(8,128)S(1)}, f32[224,128]{1,0:T(8,128)S(1)}, u32[]{:S(2)}, u32[]{:S(2)}) %collective-permute-start.32) | collective-permute-done | bytes 114720 | tf_op jit(solution)/shard_map/ppermute | solution.py:395
  25.6 3.0 %collective-permute-done.33.refs_7_ = f32[224,128]{1,0:T(8,128)S(1)} collective-permute-done((f32[224,128]{1,0:T(8,128)S(1)}, f32[224,128]{1,0:T(8,128)S(1)}, u32[]{:S(2)}, u32[]{:S(2)}) %collective-permute-start.33) | collective-permute-done | bytes 114720 | tf_op jit(solution)/shard_map/ppermute | solution.py:395
  29.4 2.3 %collective-permute-start.34 = (f32[520,128]{1,0:T(8,128)S(1)}, f32[520,128]{1,0:T(8,128)S(1)}, u32[]{:S(2)}, u32[]{:S(2)}) collective-permute-start(f32[520,128]{1,0:T(8,128)S(1)} %collect.7), channel_id=1, source_target_pairs={{0,16},{1,17},{2,18},{3,19},{4,20},{5,21},{6,22},{7,23},{8,24},{9,... | collective-permute-start | bytes 798728 | tf_op jit(solution)/shard_map/ppermute | solution.py:395
  33.3 1.8 %collective-permute-start.22 = (f32[224,128]{1,0:T(8,128)S(1)}, f32[224,128]{1,0:T(8,128)S(1)}, u32[]{:S(2)}, u32[]{:S(2)}) collective-permute-start(f32[224,128]{1,0:T(8,128)S(1)} %get-tuple-element.104), channel_id=1, source_target_pairs={{0,6},{1,7},{2,4},{3,5},{4,2},{5,3},{6,0},{7,1},{8,14},{9,15},{10,... | collective-permute-start | bytes 344072 | tf_op jit(solution)/shard_map/ppermute | solution.py:395
  35.1 1.2 %collective-permute-start.23 = (f32[224,128]{1,0:T(8,128)S(1)}, f32[224,128]{1,0:T(8,128)S(1)}, u32[]{:S(2)}, u32[]{:S(2)}) collective-permute-start(f32[224,128]{1,0:T(8,128)S(1)} %get-tuple-element.105), channel_id=1, source_target_pairs={{0,8},{1,9},{2,10},{3,11},{4,12},{5,13},{6,14},{7,15},{8,0},{9,1},... | collective-permute-start | bytes 344072 | tf_op jit(solution)/shard_map/ppermute | solution.py:395
  36.3 1.3 %collective-permute-start.24 = (f32[224,128]{1,0:T(8,128)S(1)}, f32[224,128]{1,0:T(8,128)S(1)}, u32[]{:S(2)}, u32[]{:S(2)}) collective-permute-start(f32[224,128]{1,0:T(8,128)S(1)} %get-tuple-element.106), channel_id=1, source_target_pairs={{0,10},{1,11},{2,8},{3,9},{4,14},{5,15},{6,12},{7,13},{8,2},{9,3},... | collective-permute-start | bytes 344072 | tf_op jit(solution)/shard_map/ppermute | solution.py:395
  38.4 3.3 %collective-permute-start.26 = (f32[224,128]{1,0:T(8,128)S(1)}, f32[224,128]{1,0:T(8,128)S(1)}, u32[]{:S(2)}, u32[]{:S(2)}) collective-permute-start(f32[224,128]{1,0:T(8,128)S(1)} %get-tuple-element.108), channel_id=1, source_target_pairs={{0,14},{1,15},{2,12},{3,13},{4,10},{5,11},{6,8},{7,9},{8,6},{9,7},... | collective-permute-start | bytes 344072 | tf_op jit(solution)/shard_map/ppermute | solution.py:395
  41.7 3.8 %collective-permute-done.24.refs_5_ = f32[224,128]{1,0:T(8,128)S(1)} collective-permute-done((f32[224,128]{1,0:T(8,128)S(1)}, f32[224,128]{1,0:T(8,128)S(1)}, u32[]{:S(2)}, u32[]{:S(2)}) %collective-permute-start.24) | collective-permute-done | bytes 114720 | tf_op jit(solution)/shard_map/ppermute | solution.py:395
  45.5 3.1 %collective-permute-done.25.refs_6_ = f32[224,128]{1,0:T(8,128)S(1)} collective-permute-done((f32[224,128]{1,0:T(8,128)S(1)}, f32[224,128]{1,0:T(8,128)S(1)}, u32[]{:S(2)}, u32[]{:S(2)}) %collective-permute-start.25) | collective-permute-done | bytes 114720 | tf_op jit(solution)/shard_map/ppermute | solution.py:395
  48.6 2.0 %collective-permute-done.26.refs_7_ = f32[224,128]{1,0:T(8,128)S(1)} collective-permute-done((f32[224,128]{1,0:T(8,128)S(1)}, f32[224,128]{1,0:T(8,128)S(1)}, u32[]{:S(2)}, u32[]{:S(2)}) %collective-permute-start.26) | collective-permute-done | bytes 114720 | tf_op jit(solution)/shard_map/ppermute | solution.py:395
  51.3 1.4 %collective-permute-start.35 = (f32[520,128]{1,0:T(8,128)S(1)}, f32[520,128]{1,0:T(8,128)S(1)}, u32[]{:S(2)}, u32[]{:S(2)}) collective-permute-start(f32[520,128]{1,0:T(8,128)S(1)} %add.9.own_ref), channel_id=1, source_target_pairs={{0,2},{1,3},{2,0},{3,1},{4,6},{5,7},{6,4},{7,5},{8,10},{9,11},{10,... | collective-permute-start | bytes 798728 | tf_op jit(solution)/shard_map/ppermute | solution.py:395
  52.8 2.6 %collective-permute-start.37 = (f32[520,128]{1,0:T(8,128)S(1)}, f32[520,128]{1,0:T(8,128)S(1)}, u32[]{:S(2)}, u32[]{:S(2)}) collective-permute-start(f32[520,128]{1,0:T(8,128)S(1)} %add.9.own_ref), channel_id=1, source_target_pairs={{0,1},{1,0},{2,3},{3,2},{4,5},{5,4},{6,7},{7,6},{8,9},{9,8},{10,11... | collective-permute-start | bytes 798728 | tf_op jit(solution)/shard_map/ppermute | solution.py:395
  55.4 1.3 %collective-permute-done.35.refs_0_ = f32[520,128]{1,0:T(8,128)S(1)} collective-permute-done((f32[520,128]{1,0:T(8,128)S(1)}, f32[520,128]{1,0:T(8,128)S(1)}, u32[]{:S(2)}, u32[]{:S(2)}) %collective-permute-start.35) | collective-permute-done | bytes 266272 | tf_op jit(solution)/shard_map/ppermute | solution.py:395
  56.7 3.7 %collective-permute-start.36 = (f32[520,128]{1,0:T(8,128)S(1)}, f32[520,128]{1,0:T(8,128)S(1)}, u32[]{:S(2)}, u32[]{:S(2)}) collective-permute-start(f32[520,128]{1,0:T(8,128)S(1)} %collective-permute-done.35.refs_0_), channel_id=1, source_target_pairs={{0,1},{1,0},{2,3},{3,2},{4,5},{5,4},{6,7},{7,6},{8,9},{9,8},{10,11... | collective-permute-start | bytes 798728 | tf_op jit(solution)/shard_map/ppermute | solution.py:395
  62.7 1.6 %shard_map.77 = (f32[512,256]{1,0:T(8,128)S(1)}, f32[1024,256]{1,0:T(8,128)S(1)}) custom-call(s32[3]{0:T(128)S(1)} %pad_add_fusion.me_ref, s32[1024]{0:T(1024)S(1)} %bitcast.37, f32[520,128]{1,0:T(8,128)S(1)} %add.9.own_ref, f32[520,128]{1,0:T(8,128)S(1)} %collective-permute-done.37.other_ref), custom_call_target="tpu_custom_call" | custom-call | tf_op jit(solution)/shard_map/pallas_call | solution.py:359
  64.4 2.8 %shard_map.78 = (f32[512,256]{1,0:T(8,128)}, f32[1024,256]{1,0:T(8,128)}) custom-call(s32[3]{0:T(128)S(1)} %pad_add_fusion.me_ref, s32[1024]{0:T(1024)S(1)} %bitcast.38, f32[520,128]{1,0:T(8,128)S(1)} %collective-permute-done.35.refs_0_, f32[520,128]{1,0:T(8,128)S(1)} %collective-permute-done.36.refs_1_, f32[512,256]{1,0:T(8,128)S(1)} %get-tuple-element.117.refs_2_, ...), custom_call_target="tpu_custom_call" | custom-call | tf_op jit(solution)/shard_map/pallas_call | solution.py:359
  (43 shorter events, 8.1 us)
Async XLA Ops:
  0.6 59.7 %copy-start = (s32[8192]{0:T(1024)S(1)}, s32[8192]{0:T(1024)}, u32[]{:S(2)}) copy-start(s32[8192]{0:T(1024)} %param.13) | copy-start | bytes 98308
  2.3 5.1 %copy-start.1 = (bf16[16384,128]{1,0:T(8,128)(2,1)S(1)}, bf16[16384,128]{1,0:T(8,128)(2,1)}, u32[]{:S(2)}) copy-start(bf16[16384,128]{1,0:T(8,128)(2,1)} %kernel_hbm.3) | copy-start | bytes 12582916
  2.3 5.1 %copy-start.3 = (s32[1,16384]{1,0:T(1,128)S(1)}, s32[1,16384]{1,0:T(1,128)}, u32[]{:S(2)}) copy-start(s32[1,16384]{1,0:T(1,128)} %param.11) | copy-start | bytes 196612
  2.3 5.1 %copy-start.4 = (bf16[16384]{0:T(1024)(128)(2,1)S(1)}, bf16[16384]{0:T(1024)(128)(2,1)}, u32[]{:S(2)}) copy-start(bf16[16384]{0:T(1024)(128)(2,1)} %param.9) | copy-start | bytes 98308
  7.4 3.6 %collective-permute-start.19 = (f32[1792,128]{1,0:T(8,128)S(1)}, f32[1792,128]{1,0:T(8,128)S(1)}, u32[]{:S(2)}, u32[]{:S(2)}) collective-permute-start(f32[1792,128]{1,0:T(8,128)S(1)} %project.7), channel_id=1, source_target_pairs={{0,1},{1,0},{2,3},{3,2},{4,5},{5,4},{6,7},{7,6},{8,9},{9,8},{10,11... | collective-permute-start | bytes 2752520 | tf_op jit(solution)/shard_map/ppermute | solution.py:395
  11.6 6.6 %collective-permute-start.27 = (f32[224,128]{1,0:T(8,128)S(1)}, f32[224,128]{1,0:T(8,128)S(1)}, u32[]{:S(2)}, u32[]{:S(2)}) collective-permute-start(f32[224,128]{1,0:T(8,128)S(1)} %get-tuple-element.110), channel_id=1, source_target_pairs={{0,2},{1,3},{2,0},{3,1},{4,6},{5,7},{6,4},{7,5},{8,10},{9,11},{10,... | collective-permute-start | bytes 344072 | tf_op jit(solution)/shard_map/ppermute | solution.py:395
  14.3 6.1 %collective-permute-start.28 = (f32[224,128]{1,0:T(8,128)S(1)}, f32[224,128]{1,0:T(8,128)S(1)}, u32[]{:S(2)}, u32[]{:S(2)}) collective-permute-start(f32[224,128]{1,0:T(8,128)S(1)} %get-tuple-element.111), channel_id=1, source_target_pairs={{0,4},{1,5},{2,6},{3,7},{4,0},{5,1},{6,2},{7,3},{8,12},{9,13},{10,... | collective-permute-start | bytes 344072 | tf_op jit(solution)/shard_map/ppermute | solution.py:395
  15.6 5.5 %collective-permute-start.29 = (f32[224,128]{1,0:T(8,128)S(1)}, f32[224,128]{1,0:T(8,128)S(1)}, u32[]{:S(2)}, u32[]{:S(2)}) collective-permute-start(f32[224,128]{1,0:T(8,128)S(1)} %get-tuple-element.112), channel_id=1, source_target_pairs={{0,6},{1,7},{2,4},{3,5},{4,2},{5,3},{6,0},{7,1},{8,14},{9,15},{10,... | collective-permute-start | bytes 344072 | tf_op jit(solution)/shard_map/ppermute | solution.py:395
  15.6 5.5 %collective-permute-start.30 = (f32[224,128]{1,0:T(8,128)S(1)}, f32[224,128]{1,0:T(8,128)S(1)}, u32[]{:S(2)}, u32[]{:S(2)}) collective-permute-start(f32[224,128]{1,0:T(8,128)S(1)} %get-tuple-element.113), channel_id=1, source_target_pairs={{0,8},{1,9},{2,10},{3,11},{4,12},{5,13},{6,14},{7,15},{8,0},{9,1},... | collective-permute-start | bytes 344072 | tf_op jit(solution)/shard_map/ppermute | solution.py:395
  17.1 5.7 %collective-permute-start.31 = (f32[224,128]{1,0:T(8,128)S(1)}, f32[224,128]{1,0:T(8,128)S(1)}, u32[]{:S(2)}, u32[]{:S(2)}) collective-permute-start(f32[224,128]{1,0:T(8,128)S(1)} %get-tuple-element.114), channel_id=1, source_target_pairs={{0,10},{1,11},{2,8},{3,9},{4,14},{5,15},{6,12},{7,13},{8,2},{9,3},... | collective-permute-start | bytes 344072 | tf_op jit(solution)/shard_map/ppermute | solution.py:395
  18.2 7.4 %collective-permute-start.32 = (f32[224,128]{1,0:T(8,128)S(1)}, f32[224,128]{1,0:T(8,128)S(1)}, u32[]{:S(2)}, u32[]{:S(2)}) collective-permute-start(f32[224,128]{1,0:T(8,128)S(1)} %get-tuple-element.115), channel_id=1, source_target_pairs={{0,12},{1,13},{2,14},{3,15},{4,8},{5,9},{6,10},{7,11},{8,4},{9,5},... | collective-permute-start | bytes 344072 | tf_op jit(solution)/shard_map/ppermute | solution.py:395
  20.4 8.2 %collective-permute-start.33 = (f32[224,128]{1,0:T(8,128)S(1)}, f32[224,128]{1,0:T(8,128)S(1)}, u32[]{:S(2)}, u32[]{:S(2)}) collective-permute-start(f32[224,128]{1,0:T(8,128)S(1)} %get-tuple-element.116), channel_id=1, source_target_pairs={{0,14},{1,15},{2,12},{3,13},{4,10},{5,11},{6,8},{7,9},{8,6},{9,7},... | collective-permute-start | bytes 344072 | tf_op jit(solution)/shard_map/ppermute | solution.py:395
  29.4 21.9 %collective-permute-start.34 = (f32[520,128]{1,0:T(8,128)S(1)}, f32[520,128]{1,0:T(8,128)S(1)}, u32[]{:S(2)}, u32[]{:S(2)}) collective-permute-start(f32[520,128]{1,0:T(8,128)S(1)} %collect.7), channel_id=1, source_target_pairs={{0,16},{1,17},{2,18},{3,19},{4,20},{5,21},{6,22},{7,23},{8,24},{9,... | collective-permute-start | bytes 798728 | tf_op jit(solution)/shard_map/ppermute | solution.py:395
  32.4 3.9 %collective-permute-start.20 = (f32[224,128]{1,0:T(8,128)S(1)}, f32[224,128]{1,0:T(8,128)S(1)}, u32[]{:S(2)}, u32[]{:S(2)}) collective-permute-start(f32[224,128]{1,0:T(8,128)S(1)} %get-tuple-element.102), channel_id=1, source_target_pairs={{0,2},{1,3},{2,0},{3,1},{4,6},{5,7},{6,4},{7,5},{8,10},{9,11},{10,... | collective-permute-start | bytes 344072 | tf_op jit(solution)/shard_map/ppermute | solution.py:395
  32.8 4.8 %collective-permute-start.21 = (f32[224,128]{1,0:T(8,128)S(1)}, f32[224,128]{1,0:T(8,128)S(1)}, u32[]{:S(2)}, u32[]{:S(2)}) collective-permute-start(f32[224,128]{1,0:T(8,128)S(1)} %get-tuple-element.103), channel_id=1, source_target_pairs={{0,4},{1,5},{2,6},{3,7},{4,0},{5,1},{6,2},{7,3},{8,12},{9,13},{10,... | collective-permute-start | bytes 344072 | tf_op jit(solution)/shard_map/ppermute | solution.py:395
  33.3 5.1 %collective-permute-start.22 = (f32[224,128]{1,0:T(8,128)S(1)}, f32[224,128]{1,0:T(8,128)S(1)}, u32[]{:S(2)}, u32[]{:S(2)}) collective-permute-start(f32[224,128]{1,0:T(8,128)S(1)} %get-tuple-element.104), channel_id=1, source_target_pairs={{0,6},{1,7},{2,4},{3,5},{4,2},{5,3},{6,0},{7,1},{8,14},{9,15},{10,... | collective-permute-start | bytes 344072 | tf_op jit(solution)/shard_map/ppermute | solution.py:395
  35.1 6.6 %collective-permute-start.23 = (f32[224,128]{1,0:T(8,128)S(1)}, f32[224,128]{1,0:T(8,128)S(1)}, u32[]{:S(2)}, u32[]{:S(2)}) collective-permute-start(f32[224,128]{1,0:T(8,128)S(1)} %get-tuple-element.105), channel_id=1, source_target_pairs={{0,8},{1,9},{2,10},{3,11},{4,12},{5,13},{6,14},{7,15},{8,0},{9,1},... | collective-permute-start | bytes 344072 | tf_op jit(solution)/shard_map/ppermute | solution.py:395
  36.3 9.2 %collective-permute-start.24 = (f32[224,128]{1,0:T(8,128)S(1)}, f32[224,128]{1,0:T(8,128)S(1)}, u32[]{:S(2)}, u32[]{:S(2)}) collective-permute-start(f32[224,128]{1,0:T(8,128)S(1)} %get-tuple-element.106), channel_id=1, source_target_pairs={{0,10},{1,11},{2,8},{3,9},{4,14},{5,15},{6,12},{7,13},{8,2},{9,3},... | collective-permute-start | bytes 344072 | tf_op jit(solution)/shard_map/ppermute | solution.py:395
  37.6 11.0 %collective-permute-start.25 = (f32[224,128]{1,0:T(8,128)S(1)}, f32[224,128]{1,0:T(8,128)S(1)}, u32[]{:S(2)}, u32[]{:S(2)}) collective-permute-start(f32[224,128]{1,0:T(8,128)S(1)} %get-tuple-element.107), channel_id=1, source_target_pairs={{0,12},{1,13},{2,14},{3,15},{4,8},{5,9},{6,10},{7,11},{8,4},{9,5},... | collective-permute-start | bytes 344072 | tf_op jit(solution)/shard_map/ppermute | solution.py:395
  38.4 12.1 %collective-permute-start.26 = (f32[224,128]{1,0:T(8,128)S(1)}, f32[224,128]{1,0:T(8,128)S(1)}, u32[]{:S(2)}, u32[]{:S(2)}) collective-permute-start(f32[224,128]{1,0:T(8,128)S(1)} %get-tuple-element.108), channel_id=1, source_target_pairs={{0,14},{1,15},{2,12},{3,13},{4,10},{5,11},{6,8},{7,9},{8,6},{9,7},... | collective-permute-start | bytes 344072 | tf_op jit(solution)/shard_map/ppermute | solution.py:395
  50.5 16.6 %copy-start.6 = (s32[1,1024]{1,0:T(1,128)S(1)}, s32[1,1024]{1,0:T(1,128)}, u32[]{:S(2)}) copy-start(s32[1,1024]{1,0:T(1,128)} %param.12) | copy-start | bytes 12292
  51.3 5.3 %collective-permute-start.35 = (f32[520,128]{1,0:T(8,128)S(1)}, f32[520,128]{1,0:T(8,128)S(1)}, u32[]{:S(2)}, u32[]{:S(2)}) collective-permute-start(f32[520,128]{1,0:T(8,128)S(1)} %add.9.own_ref), channel_id=1, source_target_pairs={{0,2},{1,3},{2,0},{3,1},{4,6},{5,7},{6,4},{7,5},{8,10},{9,11},{10,... | collective-permute-start | bytes 798728 | tf_op jit(solution)/shard_map/ppermute | solution.py:395
  52.8 9.9 %collective-permute-start.37 = (f32[520,128]{1,0:T(8,128)S(1)}, f32[520,128]{1,0:T(8,128)S(1)}, u32[]{:S(2)}, u32[]{:S(2)}) collective-permute-start(f32[520,128]{1,0:T(8,128)S(1)} %add.9.own_ref), channel_id=1, source_target_pairs={{0,1},{1,0},{2,3},{3,2},{4,5},{5,4},{6,7},{7,6},{8,9},{9,8},{10,11... | collective-permute-start | bytes 798728 | tf_op jit(solution)/shard_map/ppermute | solution.py:395
  56.7 7.7 %collective-permute-start.36 = (f32[520,128]{1,0:T(8,128)S(1)}, f32[520,128]{1,0:T(8,128)S(1)}, u32[]{:S(2)}, u32[]{:S(2)}) collective-permute-start(f32[520,128]{1,0:T(8,128)S(1)} %collective-permute-done.35.refs_0_), channel_id=1, source_target_pairs={{0,1},{1,0},{2,3},{3,2},{4,5},{5,4},{6,7},{7,6},{8,9},{9,8},{10,11... | collective-permute-start | bytes 798728 | tf_op jit(solution)/shard_map/ppermute | solution.py:395
  (1 other events, 5.1 us)

commit v3 on v2

--- a/solution.py
+++ b/solution.py
@@ -114,8 +114,9 @@
 
 
 def project_kernel(
-    steps, cap, own, me_ref, ends_ref, place_ref, kernel_hbm, thermal_ref, kinetic_ref, slot_ref, head_ref,
-    out_ref, kernel_ref, partial_ref, stage_ref, factor_s, in_sem
+    steps, cap, me_ref, ends_ref, place_ref, kernel_hbm, thermal_ref, kinetic_ref, slot_ref, head_ref,
+    far_own_ref, near_own_ref, far_other_ref, near_other_ref,
+    kernel_ref, own_ref, other_ref, own_stage, other_stage, own_s, other_s, in_sem
 ):
     entries, _ = kernel_ref.shape
     part = entries // steps
@@ -130,10 +131,11 @@
 
     for step in range(steps):
         load(step).start()
-    partial_ref[...] = jnp.zeros_like(partial_ref)
-    stage_ref[...] = jnp.zeros_like(stage_ref)
-    first_channel = (me_ref[2] == 0) == own
-    factor_s[...] = jnp.where(first_channel, thermal_ref[...].astype(jnp.float32), kinetic_ref[...].astype(jnp.float32))
+    for ref in (own_ref, other_ref, own_stage, other_stage):
+        ref[...] = jnp.zeros_like(ref)
+    thermal, kinetic = thermal_ref[...].astype(jnp.float32), kinetic_ref[...].astype(jnp.float32)
+    own_s[...] = jnp.where(me_ref[2] == 0, thermal, kinetic)
+    other_s[...] = jnp.where(me_ref[2] == 0, kinetic, thermal)
     line = iota((WINDOW, LANES), 0)
 
     def first(group):
@@ -143,13 +145,19 @@
         return ends_ref[total + group * lines + lines - 1] - first(group)
 
     def add(group, base):
-        row = []
+        own, other = [], []
         for r in range(lines):
             at = pl.ds(group * lines + r, 1)
-            row.append(jnp.where(line == slot_ref[at, :] - base, factor_s[at, :], 0.0))
-        weights = jnp.concatenate(row, axis=1).astype(jnp.bfloat16)
+            match = line == slot_ref[at, :] - base
+            own.append(jnp.where(match, own_s[at, :], 0.0))
+            other.append(jnp.where(match, other_s[at, :], 0.0))
+        weights = jnp.concatenate(
+            [jnp.concatenate(own, axis=1), jnp.concatenate(other, axis=1)], axis=0
+        ).astype(jnp.bfloat16)
         sums = dot(weights, kernel_ref[pl.ds(pl.multiple_of(group * GROUP, GROUP), GROUP), :])
-        partial_ref[pl.ds(pl.multiple_of(base, 8), WINDOW), :] += sums
+        window = pl.ds(pl.multiple_of(base, 8), WINDOW)
+        own_ref[window, :] += sums[:WINDOW]
+        other_ref[window, :] += sums[WINDOW:]
 
     def turn(step, most):
         load(step).wait()
@@ -177,31 +185,38 @@
     def move(i, carry):
         for u in range(unroll):
             s = i * unroll + u
-            stage_ref[pl.ds(place_ref[s], 1), :] = partial_ref[pl.ds(s, 1), :]
+            to = place_ref[s]
+            own_stage[pl.ds(to, 1), :] = own_ref[pl.ds(s, 1), :]
+            other_stage[pl.ds(to, 1), :] = other_ref[pl.ds(s, 1), :]
         return carry
 
     lax.fori_loop(0, slots // unroll, move, 0)
     size = cap + HEAD
-    for k in range(head_ref.shape[0] // HEAD):
-        out_ref[k * size : k * size + cap, :] = stage_ref[k * size : k * size + cap, :]
-        out_ref[k * size + cap : (k + 1) * size, :] = head_ref[k * HEAD : (k + 1) * HEAD, :]
-
-
-def project(me, kernel, factors, slot, ends, place, head, cap, own):
+    classes = head_ref.shape[0] // HEAD
+    count = classes // 2
+    for near, far, stage in ((near_own_ref, far_own_ref, own_stage), (near_other_ref, far_other_ref, other_stage)):
+        for k in range(classes):
+            out, at = (near, k * size) if k < count else (far, (k - count) * size)
+            out[at : at + cap, :] = stage[k * size : k * size + cap, :]
+            out[at + cap : at + size, :] = head_ref[k * HEAD : (k + 1) * HEAD, :]
+
+
+def project(me, kernel, factors, slot, ends, place, head, cap):
     entries, pixels = kernel.shape
     slots = place.shape[0]
     steps = 4
     rows = head.shape[0] // HEAD * (cap + HEAD)
-    return pl.pallas_call(
-        functools.partial(project_kernel, steps, cap, own),
+    partial = pltpu.VMEM((slots + WINDOW, pixels), jnp.float32)
+    stage = pltpu.VMEM((rows + HEAD, pixels), jnp.float32)
+    factor = pltpu.VMEM(slot.shape, jnp.float32)
+    return pl.pallas_call(
+        functools.partial(project_kernel, steps, cap),
         in_specs=[SMEM, SMEM, SMEM, HBM, VMEM, VMEM, VMEM, VMEM],
-        out_specs=VMEM,
-        out_shape=jax.ShapeDtypeStruct((rows, pixels), jnp.float32),
+        out_specs=[VMEM] * 4,
+        out_shape=[jax.ShapeDtypeStruct((rows // 2, pixels), jnp.float32)] * 4,
         scratch_shapes=[
             pltpu.VMEM((entries, pixels), kernel.dtype),
-            pltpu.VMEM((slots + WINDOW, pixels), jnp.float32),
-            pltpu.VMEM((rows + HEAD, pixels), jnp.float32),
-            pltpu.VMEM(slot.shape, jnp.float32),
+            partial, partial, stage, stage, factor, factor,
             pltpu.SemaphoreType.DMA((steps,)),
         ],
         compiler_params=ROOM,
@@ -209,18 +224,19 @@
     )(me, ends, place, kernel, *factors, slot, head)
 
 
-def pack_kernel(first, size, me_ref, mine_ref, other_ref, *outs):
+def pack_kernel(size, me_ref, mine_ref, other_ref, *outs):
     core = me_ref[2]
     for at, rows in ((core, mine_ref), (1 - core, other_ref)):
         at = pl.ds(pl.multiple_of(at * size, 8), size)
         for k, out in enumerate(outs):
-            out[at, :] = rows[(first + k) * size : (first + k + 1) * size, :]
-
-
-def pack(me, mine, other, first, count, size):
+            out[at, :] = rows[k * size : (k + 1) * size, :]
+
+
+def pack(me, mine, other, size):
+    count = mine.shape[0] // size
     out = jax.ShapeDtypeStruct((2 * size, mine.shape[1]), jnp.float32)
     return pl.pallas_call(
-        functools.partial(pack_kernel, first, size),
+        functools.partial(pack_kernel, size),
         in_specs=[SMEM, VMEM, VMEM],
         out_specs=[VMEM] * count,
         out_shape=[out] * count,
@@ -304,11 +320,13 @@
     )(me, owners)
 
 
-def fill_rows(row_ref, table_ref, owned_ref, start, end):
+def fill_rows(row_ref, moves, start, end, shift):
     unroll = 8
 
     def one(r):
-        owned_ref[pl.ds(r, 1), :] = table_ref[pl.ds(row_ref[r], 1), :]
+        at = pl.ds(row_ref[r] - shift, 1)
+        for table, rows in moves:
+            rows[pl.ds(r, 1), :] = table[at, :]
 
     def group(i, carry):
         for u in range(unroll):
@@ -324,48 +342,85 @@
     lax.fori_loop(start + groups * unroll, end, rest, 0)
 
 
-def place_part(m, part_tiles, me_ref, own_ref, other_ref, map_ref):
-    pixels = own_ref.shape[1]
-    own, other = own_ref[:part_tiles, :], other_ref[:part_tiles, :]
-    at = pl.ds(pl.multiple_of((me_ref[1] ^ m) * part_tiles, part_tiles), part_tiles)
-    map_ref[at, :pixels] = jnp.where(me_ref[2] == 0, own, other)
-    map_ref[at, pixels:] = jnp.where(me_ref[2] == 0, other, own)
-
-
-def early_kernel(parts, me_ref, row_ref, own_ref, other_ref, owned_ref, map_ref):
-    most = owned_ref.shape[0]
-    owned_ref[...] = jnp.zeros_like(owned_ref)
-    place_part(0, map_ref.shape[0] // parts, me_ref, own_ref, other_ref, map_ref)
-    x = me_ref[1]
-    fill_rows(row_ref, map_ref, owned_ref, row_ref[most + x], row_ref[most + x + 1])
-
-
-def late_kernel(parts, me_ref, row_ref, *refs):
-    pieces, (early_owned, early_map, owned_ref, map_ref) = refs[:-4], refs[-4:]
-    most = owned_ref.shape[0]
-    part_tiles = map_ref.shape[0] // parts
-    x = me_ref[1]
-    mine = pl.ds(pl.multiple_of(x * part_tiles, part_tiles), part_tiles)
-    owned_ref[...] = early_owned[...]
-    map_ref[mine, :] = early_map[mine, :]
-    for m in range(1, parts):
-        place_part(m, part_tiles, me_ref, pieces[2 * m - 2], pieces[2 * m - 1], map_ref)
-    fill_rows(row_ref, map_ref, owned_ref, 0, row_ref[most + x])
-    fill_rows(row_ref, map_ref, owned_ref, row_ref[most + x + 1], row_ref[most + parts])
-
-
-def finish(kernel, me, rows, pieces, most, block, parts):
-    width = 2 * pieces[0].shape[1]
-    return pl.pallas_call(
-        functools.partial(kernel, parts),
-        in_specs=[SMEM, SMEM] + [VMEM] * len(pieces),
+def fill_part(m, me_ref, row_ref, moves):
+    most = moves[0][1].shape[0]
+    tiles = moves[0][0].shape[0] - HEAD
+    part = me_ref[1] ^ m
+    fill_rows(row_ref, moves, row_ref[most + part], row_ref[most + part + 1], part * tiles)
+
+
+def early_kernel(me_ref, row_ref, own_ref, other_ref, own_rows, other_rows, flag_ref):
+    tiles = own_ref.shape[0] - HEAD
+    flag_ref[0] = jnp.max(own_ref[tiles:, :]).astype(jnp.int32)
+    own_rows[...] = jnp.zeros_like(own_rows)
+    other_rows[...] = jnp.zeros_like(other_rows)
+    fill_part(0, me_ref, row_ref, ((own_ref, own_rows), (other_ref, other_rows)))
+
+
+def early(me, rows, own, other, most):
+    pixels = own.shape[1]
+    out = jax.ShapeDtypeStruct((most, pixels), jnp.float32)
+    return pl.pallas_call(
+        early_kernel,
+        in_specs=[SMEM, SMEM, VMEM, VMEM],
+        out_specs=[VMEM, VMEM, SMEM],
+        out_shape=[out, out, jax.ShapeDtypeStruct((1,), jnp.int32)],
+        compiler_params=ROOM,
+        name="early",
+    )(me, rows, own, other)
+
+
+def middle_kernel(me_ref, row_ref, before_ref, *refs):
+    pieces, rows_ref = refs[:-1], refs[-1]
+    rows_ref[...] = before_ref[...]
+    for m, piece in enumerate(pieces, 1):
+        fill_part(m, me_ref, row_ref, ((piece, rows_ref),))
+
+
+def middle(me, rows, before, pieces):
+    return pl.pallas_call(
+        middle_kernel,
+        in_specs=[SMEM, SMEM, VMEM] + [VMEM] * len(pieces),
+        out_specs=VMEM,
+        out_shape=jax.ShapeDtypeStruct(before.shape, jnp.float32),
+        compiler_params=ROOM,
+        name="middle",
+    )(me, rows, before, *pieces)
+
+
+def late_kernel(me_ref, row_ref, own_rows, before_ref, *refs):
+    pieces, (owned_ref, map_ref, other_rows) = refs[:-3], refs[-3:]
+    tiles, pixels = pieces[0].shape[0] - HEAD, pieces[0].shape[1]
+    lower = me_ref[2] == 0
+
+    def put(ref, at, own, other):
+        ref[at, :pixels] = jnp.where(lower, own, other)
+        ref[at, pixels:] = jnp.where(lower, other, own)
+
+    other_rows[...] = before_ref[...]
+    for m in range(len(pieces) // 2):
+        own, other = pieces[2 * m], pieces[2 * m + 1]
+        at = pl.ds(pl.multiple_of((me_ref[1] ^ m) * tiles, tiles), tiles)
+        put(map_ref, at, own[:tiles, :], other[:tiles, :])
+        if m:
+            fill_part(m, me_ref, row_ref, ((other, other_rows),))
+    put(owned_ref, slice(None), own_rows[...], other_rows[...])
+
+
+def late(me, rows, own_rows, before, pieces, block):
+    most, pixels = own_rows.shape
+    return pl.pallas_call(
+        late_kernel,
+        in_specs=[SMEM, SMEM] + [VMEM] * (2 + len(pieces)),
         out_specs=[VMEM, VMEM],
         out_shape=[
-            jax.ShapeDtypeStruct((most, width), jnp.float32),
-            jax.ShapeDtypeStruct((block, width), jnp.float32),
+            jax.ShapeDtypeStruct((most, 2 * pixels), jnp.float32),
+            jax.ShapeDtypeStruct((block, 2 * pixels), jnp.float32),
         ],
-        compiler_params=ROOM,
-    )(me, rows, *pieces)
+        scratch_shapes=[pltpu.VMEM((most, pixels), jnp.float32)],
+        compiler_params=ROOM,
+        name="late",
+    )(me, rows, own_rows, before, *pieces)
 
 
 def shards(kernel, pressure, velocity, entry_slot, slot_tile, tile_owner):
@@ -396,29 +451,28 @@
 
     def exchange(cap):
         size = cap + HEAD
-        count = half * parts
         place, ends, head = plan(me, tiles, slot, vols, parts, block, cap)
-        place, ends = place.reshape(-1), ends.reshape(-1)
-        given = project(me, kernel, factors, slot, ends, place, head, cap, False)
-        taken = send(given, core_step=1)
-        held = project(me, kernel, factors, slot, ends, place, head, cap, True)
-
-        def gather(first):
-            messages = list(pack(me, held, taken, first, count, size))
-            for k in reversed(range(1, count)):
+        far, near, far_other, near_other = project(
+            me, kernel, factors, slot, ends.reshape(-1), place.reshape(-1), head, cap
+        )
+
+        def gather(own, other):
+            taken = send(other, core_step=1)
+            messages = list(pack(me, own, taken, size))
+            for k in reversed(range(1, len(messages))):
                 messages[k] = send(messages[k], k // parts, k % parts)
             return collect(messages, part_tiles)
 
-        far = send(gather(count), vol_step=half)
-        mine = gather(0) + far
+        crossed = send(gather(far, far_other), vol_step=half)
+        mine = gather(near, near_other) + crossed
         other = send(mine, core_step=1)
-        early = finish(early_kernel, me, rows, [mine, other], most_owned, block, parts)
-        pieces = []
-        for m in range(1, parts):
-            piece = send(mine, part_step=m)
+        own_rows, other_rows, flag = early(me, rows, mine, other, most_owned)
+        across = [send(mine, part_step=m) for m in range(1, parts)]
+        pieces = [mine, other]
+        for piece in across:
             pieces += [piece, send(piece, core_step=1)]
-        full = finish(late_kernel, me, rows, [*pieces, *early], most_owned, block, parts)
-        return mine[part_tiles, 0] > 0, *full
+        own_rows = middle(me, rows, own_rows, across)
+        return flag[0] > 0, *late(me, rows, own_rows, other_rows, pieces, block)
 
     result = exchange(most_rows * 13 // 32 // 8 * 8)
 

time: 67.3 us -> 66.3 us (0.985)
  the two profiles are of different devices: /device:TPU:1 before, /device:TPU:0 now
where the time goes in v3:
time: 66.3 us; the launch traced here: 65.1 us
  starting transfers between devices  27 us (41%)
  waiting for transfers between devices  21.7 us (33%)
  Pallas kernels  14.8 us (22%)
  between operations  1.47 us (2%)
    ppermute x20, starting transfers between devices, send(): lax.ppermute(x, ('vol', 'pix'), [(d, d ^ step) for d in range(vols * pixs)])  27 us
    ppermute x20, waiting for transfers between devices, send(): lax.ppermute(x, ('vol', 'pix'), [(d, d ^ step) for d in range(vols * pixs)])  21.7 us
    pallas_call x1, Pallas kernels, project(): pl.pallas_call(functools.partial(project_kernel, steps, cap), in_specs=[S...  5.14 us
    pallas_call x1, Pallas kernels, late(): pl.pallas_call(late_kernel, in_specs=[SMEM, SMEM] + [VMEM] * (2 + len(pie...  2.03 us
    pallas_call x1, Pallas kernels, plan(): pl.pallas_call(functools.partial(plan_kernel, vols, parts, block, cap), i...  1.58 us
    pallas_call x2, Pallas kernels, collect(): pl.pallas_call(functools.partial(collect_kernel, rows // 2, part_tiles),...  1.43 us
    pallas_call x1, Pallas kernels, early(): pl.pallas_call(early_kernel, in_specs=[SMEM, SMEM, VMEM, VMEM], out_specs...  1.41 us
  transfers between devices with their start and end apart: 20, of which 12 were waited for; matrix products, arithmetic and copies ran while one was open for 0% of the time, Pallas kernels for 9%

profile of v3, /device:TPU:0, one launch (start us, length us, event | category | flops | bytes accessed | tf_op | source)
XLA Modules:
  0.0 65.1 jit_solution(7074247639167201135)
XLA Ops:
  0.7 1.6 %plan.3 = (s32[8,128]{1,0:T(8,128)S(1)}, s32[8,128]{1,0:T(8,128)S(1)}, f32[128,128]{1,0:T(8,128)S(1)}) custom-call(s32[3]{0:T(128)S(1)} %pad_add_fusion.me_ref, s32[8,128]{1,0:T(8,128)} %bitcast.34, s32[128,128]{1,0:T(8,128)} %bitcast.23), custom_call_target="tpu_custom_call" | custom-call | tf_op jit(solution)/shard_map/plan/pallas_call | solution.py:102
  2.3 5.1 %project.3 = (f32[896,128]{1,0:T(8,128)S(1)}, f32[896,128]{1,0:T(8,128)S(1)}, f32[896,128]{1,0:T(8,128)S(1)}, f32[896,128]{1,0:T(8,128)S(1)}) custom-call(s32[3]{0:T(128)S(1)} %pad_add_fusion.me_ref, s32[1024]{0:T(1024)S(1)} %bitcast.22, s32[1024]{0:T(1024)S(1)} %bitcast.21, bf16[16384,128]{1,0:T(8,128)(2,1)} %kernel_hbm.1, bf16[128,128]{1,0:T(8,128)(2,1)} %bitcast.30, ...), custom_call_target="tpu_custom_call" | custom-call | tf_op jit(solution)/shard_map/project/pallas_call | solution.py:212
  8.1 1.4 %collective-permute-done.28.other_ref = f32[896,128]{1,0:T(8,128)S(1)} collective-permute-done((f32[896,128]{1,0:T(8,128)S(1)}, f32[896,128]{1,0:T(8,128)S(1)}, u32[]{:S(2)}, u32[]{:S(2)}) %collective-permute-start.28) | collective-permute-done | bytes 458784 | tf_op jit(solution)/shard_map/ppermute | solution.py:450
  10.1 2.9 %collective-permute-start.29 = (f32[224,128]{1,0:T(8,128)S(1)}, f32[224,128]{1,0:T(8,128)S(1)}, u32[]{:S(2)}, u32[]{:S(2)}) collective-permute-start(f32[224,128]{1,0:T(8,128)S(1)} %get-tuple-element.123), channel_id=1, source_target_pairs={{0,2},{1,3},{2,0},{3,1},{4,6},{5,7},{6,4},{7,5},{8,10},{9,11},{10,... | collective-permute-start | bytes 344072 | tf_op jit(solution)/shard_map/ppermute | solution.py:450
  13.0 1.5 %collective-permute-start.30 = (f32[224,128]{1,0:T(8,128)S(1)}, f32[224,128]{1,0:T(8,128)S(1)}, u32[]{:S(2)}, u32[]{:S(2)}) collective-permute-start(f32[224,128]{1,0:T(8,128)S(1)} %get-tuple-element.124), channel_id=1, source_target_pairs={{0,4},{1,5},{2,6},{3,7},{4,0},{5,1},{6,2},{7,3},{8,12},{9,13},{10,... | collective-permute-start | bytes 344072 | tf_op jit(solution)/shard_map/ppermute | solution.py:450
  14.5 2.0 %collective-permute-start.32 = (f32[224,128]{1,0:T(8,128)S(1)}, f32[224,128]{1,0:T(8,128)S(1)}, u32[]{:S(2)}, u32[]{:S(2)}) collective-permute-start(f32[224,128]{1,0:T(8,128)S(1)} %get-tuple-element.126), channel_id=1, source_target_pairs={{0,8},{1,9},{2,10},{3,11},{4,12},{5,13},{6,14},{7,15},{8,0},{9,1},... | collective-permute-start | bytes 344072 | tf_op jit(solution)/shard_map/ppermute | solution.py:450
  16.6 3.4 %collective-permute-start.33 = (f32[224,128]{1,0:T(8,128)S(1)}, f32[224,128]{1,0:T(8,128)S(1)}, u32[]{:S(2)}, u32[]{:S(2)}) collective-permute-start(f32[224,128]{1,0:T(8,128)S(1)} %get-tuple-element.127), channel_id=1, source_target_pairs={{0,10},{1,11},{2,8},{3,9},{4,14},{5,15},{6,12},{7,13},{8,2},{9,3},... | collective-permute-start | bytes 344072 | tf_op jit(solution)/shard_map/ppermute | solution.py:450
  20.4 2.5 %collective-permute-start.34 = (f32[224,128]{1,0:T(8,128)S(1)}, f32[224,128]{1,0:T(8,128)S(1)}, u32[]{:S(2)}, u32[]{:S(2)}) collective-permute-start(f32[224,128]{1,0:T(8,128)S(1)} %get-tuple-element.128), channel_id=1, source_target_pairs={{0,12},{1,13},{2,14},{3,15},{4,8},{5,9},{6,10},{7,11},{8,4},{9,5},... | collective-permute-start | bytes 344072 | tf_op jit(solution)/shard_map/ppermute | solution.py:450
  22.9 1.5 %collective-permute-done.33.refs_5_ = f32[224,128]{1,0:T(8,128)S(1)} collective-permute-done((f32[224,128]{1,0:T(8,128)S(1)}, f32[224,128]{1,0:T(8,128)S(1)}, u32[]{:S(2)}, u32[]{:S(2)}) %collective-permute-start.33) | collective-permute-done | bytes 114720 | tf_op jit(solution)/shard_map/ppermute | solution.py:450
  24.4 3.6 %collective-permute-done.34.refs_6_ = f32[224,128]{1,0:T(8,128)S(1)} collective-permute-done((f32[224,128]{1,0:T(8,128)S(1)}, f32[224,128]{1,0:T(8,128)S(1)}, u32[]{:S(2)}, u32[]{:S(2)}) %collective-permute-start.34) | collective-permute-done | bytes 114720 | tf_op jit(solution)/shard_map/ppermute | solution.py:450
  28.0 1.5 %collective-permute-done.35.refs_7_ = f32[224,128]{1,0:T(8,128)S(1)} collective-permute-done((f32[224,128]{1,0:T(8,128)S(1)}, f32[224,128]{1,0:T(8,128)S(1)}, u32[]{:S(2)}, u32[]{:S(2)}) %collective-permute-start.35) | collective-permute-done | bytes 114720 | tf_op jit(solution)/shard_map/ppermute | solution.py:450
  30.2 2.7 %collective-permute-start.36 = (f32[520,128]{1,0:T(8,128)S(1)}, f32[520,128]{1,0:T(8,128)S(1)}, u32[]{:S(2)}, u32[]{:S(2)}) collective-permute-start(f32[520,128]{1,0:T(8,128)S(1)} %collect.7), channel_id=1, source_target_pairs={{0,16},{1,17},{2,18},{3,19},{4,20},{5,21},{6,22},{7,23},{8,24},{9,... | collective-permute-start | bytes 798728 | tf_op jit(solution)/shard_map/ppermute | solution.py:450
  35.1 1.9 %collective-permute-start.23 = (f32[224,128]{1,0:T(8,128)S(1)}, f32[224,128]{1,0:T(8,128)S(1)}, u32[]{:S(2)}, u32[]{:S(2)}) collective-permute-start(f32[224,128]{1,0:T(8,128)S(1)} %get-tuple-element.115), channel_id=1, source_target_pairs={{0,6},{1,7},{2,4},{3,5},{4,2},{5,3},{6,0},{7,1},{8,14},{9,15},{10,... | collective-permute-start | bytes 344072 | tf_op jit(solution)/shard_map/ppermute | solution.py:450
  37.0 1.1 %collective-permute-start.24 = (f32[224,128]{1,0:T(8,128)S(1)}, f32[224,128]{1,0:T(8,128)S(1)}, u32[]{:S(2)}, u32[]{:S(2)}) collective-permute-start(f32[224,128]{1,0:T(8,128)S(1)} %get-tuple-element.116), channel_id=1, source_target_pairs={{0,8},{1,9},{2,10},{3,11},{4,12},{5,13},{6,14},{7,15},{8,0},{9,1},... | collective-permute-start | bytes 344072 | tf_op jit(solution)/shard_map/ppermute | solution.py:450
  38.5 1.9 %collective-permute-start.25 = (f32[224,128]{1,0:T(8,128)S(1)}, f32[224,128]{1,0:T(8,128)S(1)}, u32[]{:S(2)}, u32[]{:S(2)}) collective-permute-start(f32[224,128]{1,0:T(8,128)S(1)} %get-tuple-element.117), channel_id=1, source_target_pairs={{0,10},{1,11},{2,8},{3,9},{4,14},{5,15},{6,12},{7,13},{8,2},{9,3},... | collective-permute-start | bytes 344072 | tf_op jit(solution)/shard_map/ppermute | solution.py:450
  41.6 2.9 %collective-permute-start.27 = (f32[224,128]{1,0:T(8,128)S(1)}, f32[224,128]{1,0:T(8,128)S(1)}, u32[]{:S(2)}, u32[]{:S(2)}) collective-permute-start(f32[224,128]{1,0:T(8,128)S(1)} %get-tuple-element.119), channel_id=1, source_target_pairs={{0,14},{1,15},{2,12},{3,13},{4,10},{5,11},{6,8},{7,9},{8,6},{9,7},... | collective-permute-start | bytes 344072 | tf_op jit(solution)/shard_map/ppermute | solution.py:450
  44.5 1.7 %collective-permute-done.24.refs_4_ = f32[224,128]{1,0:T(8,128)S(1)} collective-permute-done((f32[224,128]{1,0:T(8,128)S(1)}, f32[224,128]{1,0:T(8,128)S(1)}, u32[]{:S(2)}, u32[]{:S(2)}) %collective-permute-start.24) | collective-permute-done | bytes 114720 | tf_op jit(solution)/shard_map/ppermute | solution.py:450
  46.2 2.5 %collective-permute-done.25.refs_5_ = f32[224,128]{1,0:T(8,128)S(1)} collective-permute-done((f32[224,128]{1,0:T(8,128)S(1)}, f32[224,128]{1,0:T(8,128)S(1)}, u32[]{:S(2)}, u32[]{:S(2)}) %collective-permute-start.25) | collective-permute-done | bytes 114720 | tf_op jit(solution)/shard_map/ppermute | solution.py:450
  48.7 1.4 %collective-permute-done.26.refs_6_ = f32[224,128]{1,0:T(8,128)S(1)} collective-permute-done((f32[224,128]{1,0:T(8,128)S(1)}, f32[224,128]{1,0:T(8,128)S(1)}, u32[]{:S(2)}, u32[]{:S(2)}) %collective-permute-start.26) | collective-permute-done | bytes 114720 | tf_op jit(solution)/shard_map/ppermute | solution.py:450
  50.1 1.6 %collective-permute-done.27.refs_7_ = f32[224,128]{1,0:T(8,128)S(1)} collective-permute-done((f32[224,128]{1,0:T(8,128)S(1)}, f32[224,128]{1,0:T(8,128)S(1)}, u32[]{:S(2)}, u32[]{:S(2)}) %collective-permute-start.27) | collective-permute-done | bytes 114720 | tf_op jit(solution)/shard_map/ppermute | solution.py:450
  53.5 5.4 %collective-permute-done.38.refs_0_.refs_2_ = f32[520,128]{1,0:T(8,128)S(1)} collective-permute-done((f32[520,128]{1,0:T(8,128)S(1)}, f32[520,128]{1,0:T(8,128)S(1)}, u32[]{:S(2)}, u32[]{:S(2)}) %collective-permute-start.38) | collective-permute-done | bytes 266272 | tf_op jit(solution)/shard_map/ppermute | solution.py:450
  58.9 1.2 %owned_rows.1 = s32[8,512]{1,0:T(8,128)S(1)} custom-call(s32[3]{0:T(128)S(1)} %pad_add_fusion.me_ref, s32[8,128]{1,0:T(8,128)S(1)} %dynamic-slice_bitcast_fusion.owner_ref), custom_call_target="tpu_custom_call" | custom-call | tf_op jit(solution)/shard_map/owned_rows/pallas_call | solution.py:313
  60.1 1.4 %early.3 = (f32[512,128]{1,0:T(8,128)S(1)}, f32[512,128]{1,0:T(8,128)S(1)}, s32[1]{0:T(128)}) custom-call(s32[3]{0:T(128)S(1)} %pad_add_fusion.me_ref, s32[1024]{0:T(1024)S(1)} %bitcast.26, f32[520,128]{1,0:T(8,128)S(1)} %add.10.own_ref.refs_0_, f32[520,128]{1,0:T(8,128)S(1)} %collective-permute-done.37.other_ref.refs_1_), custom_call_target="tpu_custom_call" | custom-call | tf_op jit(solution)/shard_map/early/pallas_call | solution.py:363
  63.1 2.0 %late.3 = (f32[512,256]{1,0:T(8,128)}, f32[1024,256]{1,0:T(8,128)}) custom-call(s32[3]{0:T(128)S(1)} %pad_add_fusion.me_ref, s32[1024]{0:T(1024)S(1)} %bitcast.28, f32[512,128]{1,0:T(8,128)S(1)} %middle.3.own_rows, f32[512,128]{1,0:T(8,128)S(1)} %get-tuple-element.132.before_ref, f32[520,128]{1,0:T(8,128)S(1)} %add.10.own_ref.refs_0_, ...), custom_call_target="tpu_custom_call" | custom-call | tf_op jit(solution)/shard_map/late/pallas_call | solution.py:412
  (42 shorter events, 8.9 us)
Async XLA Ops:
  0.6 58.3 %copy-start = (s32[8192]{0:T(1024)S(1)}, s32[8192]{0:T(1024)}, u32[]{:S(2)}) copy-start(s32[8192]{0:T(1024)} %param.13) | copy-start | bytes 98308
  7.5 2.0 %collective-permute-start.28 = (f32[896,128]{1,0:T(8,128)S(1)}, f32[896,128]{1,0:T(8,128)S(1)}, u32[]{:S(2)}, u32[]{:S(2)}) collective-permute-start(f32[896,128]{1,0:T(8,128)S(1)} %get-tuple-element.121), channel_id=1, source_target_pairs={{0,1},{1,0},{2,3},{3,2},{4,5},{5,4},{6,7},{7,6},{8,9},{9,8},{10,11... | collective-permute-start | bytes 1376264 | tf_op jit(solution)/shard_map/ppermute | solution.py:450
  8.0 24.8 %collective-permute-start.20 = (f32[896,128]{1,0:T(8,128)S(1)}, f32[896,128]{1,0:T(8,128)S(1)}, u32[]{:S(2)}, u32[]{:S(2)}) collective-permute-start(f32[896,128]{1,0:T(8,128)S(1)} %get-tuple-element.111), channel_id=1, source_target_pairs={{0,1},{1,0},{2,3},{3,2},{4,5},{5,4},{6,7},{7,6},{8,9},{9,8},{10,11... | collective-permute-start | bytes 1376264 | tf_op jit(solution)/shard_map/ppermute | solution.py:450
  10.1 6.5 %collective-permute-start.29 = (f32[224,128]{1,0:T(8,128)S(1)}, f32[224,128]{1,0:T(8,128)S(1)}, u32[]{:S(2)}, u32[]{:S(2)}) collective-permute-start(f32[224,128]{1,0:T(8,128)S(1)} %get-tuple-element.123), channel_id=1, source_target_pairs={{0,2},{1,3},{2,0},{3,1},{4,6},{5,7},{6,4},{7,5},{8,10},{9,11},{10,... | collective-permute-start | bytes 344072 | tf_op jit(solution)/shard_map/ppermute | solution.py:450
  13.0 7.4 %collective-permute-start.30 = (f32[224,128]{1,0:T(8,128)S(1)}, f32[224,128]{1,0:T(8,128)S(1)}, u32[]{:S(2)}, u32[]{:S(2)}) collective-permute-start(f32[224,128]{1,0:T(8,128)S(1)} %get-tuple-element.124), channel_id=1, source_target_pairs={{0,4},{1,5},{2,6},{3,7},{4,0},{5,1},{6,2},{7,3},{8,12},{9,13},{10,... | collective-permute-start | bytes 344072 | tf_op jit(solution)/shard_map/ppermute | solution.py:450
  14.5 8.4 %collective-permute-start.31 = (f32[224,128]{1,0:T(8,128)S(1)}, f32[224,128]{1,0:T(8,128)S(1)}, u32[]{:S(2)}, u32[]{:S(2)}) collective-permute-start(f32[224,128]{1,0:T(8,128)S(1)} %get-tuple-element.125), channel_id=1, source_target_pairs={{0,6},{1,7},{2,4},{3,5},{4,2},{5,3},{6,0},{7,1},{8,14},{9,15},{10,... | collective-permute-start | bytes 344072 | tf_op jit(solution)/shard_map/ppermute | solution.py:450
  14.5 8.4 %collective-permute-start.32 = (f32[224,128]{1,0:T(8,128)S(1)}, f32[224,128]{1,0:T(8,128)S(1)}, u32[]{:S(2)}, u32[]{:S(2)}) collective-permute-start(f32[224,128]{1,0:T(8,128)S(1)} %get-tuple-element.126), channel_id=1, source_target_pairs={{0,8},{1,9},{2,10},{3,11},{4,12},{5,13},{6,14},{7,15},{8,0},{9,1},... | collective-permute-start | bytes 344072 | tf_op jit(solution)/shard_map/ppermute | solution.py:450
  16.6 7.8 %collective-permute-start.33 = (f32[224,128]{1,0:T(8,128)S(1)}, f32[224,128]{1,0:T(8,128)S(1)}, u32[]{:S(2)}, u32[]{:S(2)}) collective-permute-start(f32[224,128]{1,0:T(8,128)S(1)} %get-tuple-element.127), channel_id=1, source_target_pairs={{0,10},{1,11},{2,8},{3,9},{4,14},{5,15},{6,12},{7,13},{8,2},{9,3},... | collective-permute-start | bytes 344072 | tf_op jit(solution)/shard_map/ppermute | solution.py:450
  20.4 7.7 %collective-permute-start.34 = (f32[224,128]{1,0:T(8,128)S(1)}, f32[224,128]{1,0:T(8,128)S(1)}, u32[]{:S(2)}, u32[]{:S(2)}) collective-permute-start(f32[224,128]{1,0:T(8,128)S(1)} %get-tuple-element.128), channel_id=1, source_target_pairs={{0,12},{1,13},{2,14},{3,15},{4,8},{5,9},{6,10},{7,11},{8,4},{9,5},... | collective-permute-start | bytes 344072 | tf_op jit(solution)/shard_map/ppermute | solution.py:450
  22.9 6.6 %collective-permute-start.35 = (f32[224,128]{1,0:T(8,128)S(1)}, f32[224,128]{1,0:T(8,128)S(1)}, u32[]{:S(2)}, u32[]{:S(2)}) collective-permute-start(f32[224,128]{1,0:T(8,128)S(1)} %get-tuple-element.129), channel_id=1, source_target_pairs={{0,14},{1,15},{2,12},{3,13},{4,10},{5,11},{6,8},{7,9},{8,6},{9,7},... | collective-permute-start | bytes 344072 | tf_op jit(solution)/shard_map/ppermute | solution.py:450
  30.2 22.2 %collective-permute-start.36 = (f32[520,128]{1,0:T(8,128)S(1)}, f32[520,128]{1,0:T(8,128)S(1)}, u32[]{:S(2)}, u32[]{:S(2)}) collective-permute-start(f32[520,128]{1,0:T(8,128)S(1)} %collect.7), channel_id=1, source_target_pairs={{0,16},{1,17},{2,18},{3,19},{4,20},{5,21},{6,22},{7,23},{8,24},{9,... | collective-permute-start | bytes 798728 | tf_op jit(solution)/shard_map/ppermute | solution.py:450
  33.5 5.0 %collective-permute-start.21 = (f32[224,128]{1,0:T(8,128)S(1)}, f32[224,128]{1,0:T(8,128)S(1)}, u32[]{:S(2)}, u32[]{:S(2)}) collective-permute-start(f32[224,128]{1,0:T(8,128)S(1)} %get-tuple-element.113), channel_id=1, source_target_pairs={{0,2},{1,3},{2,0},{3,1},{4,6},{5,7},{6,4},{7,5},{8,10},{9,11},{10,... | collective-permute-start | bytes 344072 | tf_op jit(solution)/shard_map/ppermute | solution.py:450
  34.4 6.0 %collective-permute-start.22 = (f32[224,128]{1,0:T(8,128)S(1)}, f32[224,128]{1,0:T(8,128)S(1)}, u32[]{:S(2)}, u32[]{:S(2)}) collective-permute-start(f32[224,128]{1,0:T(8,128)S(1)} %get-tuple-element.114), channel_id=1, source_target_pairs={{0,4},{1,5},{2,6},{3,7},{4,0},{5,1},{6,2},{7,3},{8,12},{9,13},{10,... | collective-permute-start | bytes 344072 | tf_op jit(solution)/shard_map/ppermute | solution.py:450
  35.1 6.5 %collective-permute-start.23 = (f32[224,128]{1,0:T(8,128)S(1)}, f32[224,128]{1,0:T(8,128)S(1)}, u32[]{:S(2)}, u32[]{:S(2)}) collective-permute-start(f32[224,128]{1,0:T(8,128)S(1)} %get-tuple-element.115), channel_id=1, source_target_pairs={{0,6},{1,7},{2,4},{3,5},{4,2},{5,3},{6,0},{7,1},{8,14},{9,15},{10,... | collective-permute-start | bytes 344072 | tf_op jit(solution)/shard_map/ppermute | solution.py:450
  37.0 9.2 %collective-permute-start.24 = (f32[224,128]{1,0:T(8,128)S(1)}, f32[224,128]{1,0:T(8,128)S(1)}, u32[]{:S(2)}, u32[]{:S(2)}) collective-permute-start(f32[224,128]{1,0:T(8,128)S(1)} %get-tuple-element.116), channel_id=1, source_target_pairs={{0,8},{1,9},{2,10},{3,11},{4,12},{5,13},{6,14},{7,15},{8,0},{9,1},... | collective-permute-start | bytes 344072 | tf_op jit(solution)/shard_map/ppermute | solution.py:450
  38.5 10.3 %collective-permute-start.25 = (f32[224,128]{1,0:T(8,128)S(1)}, f32[224,128]{1,0:T(8,128)S(1)}, u32[]{:S(2)}, u32[]{:S(2)}) collective-permute-start(f32[224,128]{1,0:T(8,128)S(1)} %get-tuple-element.117), channel_id=1, source_target_pairs={{0,10},{1,11},{2,8},{3,9},{4,14},{5,15},{6,12},{7,13},{8,2},{9,3},... | collective-permute-start | bytes 344072 | tf_op jit(solution)/shard_map/ppermute | solution.py:450
  40.4 9.7 %collective-permute-start.26 = (f32[224,128]{1,0:T(8,128)S(1)}, f32[224,128]{1,0:T(8,128)S(1)}, u32[]{:S(2)}, u32[]{:S(2)}) collective-permute-start(f32[224,128]{1,0:T(8,128)S(1)} %get-tuple-element.118), channel_id=1, source_target_pairs={{0,12},{1,13},{2,14},{3,15},{4,8},{5,9},{6,10},{7,11},{8,4},{9,5},... | collective-permute-start | bytes 344072 | tf_op jit(solution)/shard_map/ppermute | solution.py:450
  41.6 10.0 %collective-permute-start.27 = (f32[224,128]{1,0:T(8,128)S(1)}, f32[224,128]{1,0:T(8,128)S(1)}, u32[]{:S(2)}, u32[]{:S(2)}) collective-permute-start(f32[224,128]{1,0:T(8,128)S(1)} %get-tuple-element.119), channel_id=1, source_target_pairs={{0,14},{1,15},{2,12},{3,13},{4,10},{5,11},{6,8},{7,9},{8,6},{9,7},... | collective-permute-start | bytes 344072 | tf_op jit(solution)/shard_map/ppermute | solution.py:450
  52.4 6.5 %collective-permute-start.38 = (f32[520,128]{1,0:T(8,128)S(1)}, f32[520,128]{1,0:T(8,128)S(1)}, u32[]{:S(2)}, u32[]{:S(2)}) collective-permute-start(f32[520,128]{1,0:T(8,128)S(1)} %add.10.own_ref.refs_0_), channel_id=1, source_target_pairs={{0,2},{1,3},{2,0},{3,1},{4,6},{5,7},{6,4},{7,5},{8,10},{9,11},{10,... | collective-permute-start | bytes 798728 | tf_op jit(solution)/shard_map/ppermute | solution.py:450
  53.5 6.7 %collective-permute-start.37 = (f32[520,128]{1,0:T(8,128)S(1)}, f32[520,128]{1,0:T(8,128)S(1)}, u32[]{:S(2)}, u32[]{:S(2)}) collective-permute-start(f32[520,128]{1,0:T(8,128)S(1)} %add.10.own_ref.refs_0_), channel_id=1, source_target_pairs={{0,1},{1,0},{2,3},{3,2},{4,5},{5,4},{6,7},{7,6},{8,9},{9,8},{10,11... | collective-permute-start | bytes 798728 | tf_op jit(solution)/shard_map/ppermute | solution.py:450
  58.9 4.1 %collective-permute-start.39 = (f32[520,128]{1,0:T(8,128)S(1)}, f32[520,128]{1,0:T(8,128)S(1)}, u32[]{:S(2)}, u32[]{:S(2)}) collective-permute-start(f32[520,128]{1,0:T(8,128)S(1)} %collective-permute-done.38.refs_0_.refs_2_), channel_id=1, source_target_pairs={{0,1},{1,0},{2,3},{3,2},{4,5},{5,4},{6,7},{7,6},{8,9},{9,8},{10,11... | collective-permute-start | bytes 798728 | tf_op jit(solution)/shard_map/ppermute | solution.py:450
  62.2 2.9 %copy-start.1 = (s32[1,16384]{1,0:T(1,128)S(1)}, s32[1,16384]{1,0:T(1,128)}, u32[]{:S(2)}) copy-start(s32[1,16384]{1,0:T(1,128)} %param.11) | copy-start | bytes 196612
  62.2 2.9 %copy-start.2 = (bf16[16384]{0:T(1024)(128)(2,1)S(1)}, bf16[16384]{0:T(1024)(128)(2,1)}, u32[]{:S(2)}) copy-start(bf16[16384]{0:T(1024)(128)(2,1)} %param.9) | copy-start | bytes 98308
  62.2 2.9 %copy-start.3 = (bf16[16384]{0:T(1024)(128)(2,1)S(1)}, bf16[16384]{0:T(1024)(128)(2,1)}, u32[]{:S(2)}) copy-start(bf16[16384]{0:T(1024)(128)(2,1)} %param.10) | copy-start | bytes 98308
  (1 other events, 2.9 us)
